TPU v7x, 1024 devices: a whole 4x8x16 slice. The times are simulated.
1024 devices in a mesh: group: 16 (over y, x_hi), expert: 32 (over z, core), dp: 2 (over x_lo).
Axes of the slice: x: 4 (x_hi: 2, x_lo: 2; x = x_hi * 2 + x_lo), y: 8, z: 16, core: 2. Of those that a mesh axis runs over, the one named last changes fastest.
Arguments:
- tokens: bfloat16 [64, 64, 7168], P(('expert', 'dp'), 'group'), may hold values from -6 to 6
- expert_ids: int32 [64, 64, 8], P(('expert', 'dp')), may hold values from 0 to 255, as said below
- gate_codes: int32 [64, 64, 8], P(('expert', 'dp')), may hold values from 1 to 1023
- w_gate: bfloat16 [32, 7168, 2048], P('expert', None, 'group'), may hold values from -0.0625 to 0.0625
- w_up: bfloat16 [32, 7168, 2048], P('expert', None, 'group'), may hold values from -0.0625 to 0.0625
- w_down: bfloat16 [32, 2048, 7168], P('expert', 'group'), may hold values from -0.125 to 0.125
Outputs:
- mixed: bfloat16 [64, 64, 7168], P(('expert', 'dp'), 'group')
Inputs may be any that keep to these rules, and one draw needn't show every extreme that they name: `expert_ids`: each token names 8 different experts, all within at most 4 of the 8 groups of 32 consecutive ids. In every set (one index of the first dimension), each expert below 32 is named by at most 4 tokens, and some expert by exactly 4; a token names at most 4 experts below 32.
All inputs are finite; a program needn't handle non-finite values.
Results may differ from a plain program's by a relative error of at most 0.015.
Values may be sent and summed in bfloat16 or wider, within the bound.
No kernel may reach another device: no remote copies, remote signals or barrier semaphores. Data moves between devices by JAX's collectives and lax.ppermute only.
A program may use at most 64 MiB of HBM per device.

v0:
```python
import jax
import jax.numpy as jnp
from jax import lax
from jax.sharding import Mesh
from jax.sharding import PartitionSpec as P

CAPG = 4
EXPERT = ("expert_0", "expert_1")
EXPERT_DP = ("expert_0", "expert_1", "dp")


def sent_to_all(shard, axis):
    length = lax.axis_size(axis)
    return lax.all_to_all(
        jnp.broadcast_to(shard[None], (length, *shard.shape)), axis, 0, 0, tiled=True
    )


def in_order(parts, dim):
    dims = list(parts.shape[1:])
    dims[dim] *= parts.shape[0]
    return jnp.moveaxis(parts, 0, dim).reshape(dims)


def gathered_copies(shard, axis, dim):
    parts = sent_to_all(shard, axis)
    return in_order(parts, dim)


def in_blocks(shard, dim, length):
    dims = shard.shape
    parts = shard.reshape(*dims[:dim], length, dims[dim] // length, *dims[dim + 1 :])
    return jnp.moveaxis(parts, dim, 0)


def turned_blocks(parts, axes, sequence):
    inside = parts.shape[1:]
    whole = parts.reshape(*(lax.axis_size(a) for a in axes), *inside)
    for k in sequence:
        whole = lax.all_to_all(whole, axes[k], k, k, tiled=True)
    return whole.reshape(-1, *inside)


def core_and_chips(shard, groups, sequence, split_dim, concat_dim):
    length = lax.axis_size(groups[0]) * lax.axis_size(groups[1])
    parts = in_blocks(shard, split_dim, length)
    return in_order(turned_blocks(parts, groups, sequence), concat_dim)


def sent_and_summed(shard, axis, dim):
    length = lax.axis_size(axis)
    parts = lax.all_to_all(in_blocks(shard, dim, length), axis, 0, 0, tiled=True)
    return jnp.sum(parts, axis=0)


def routing(expert_ids, gate_codes, experts, capacity):
    codes = gate_codes.astype(jnp.float32)
    gates = 2.5 * codes / jnp.sum(codes, axis=-1, keepdims=True)
    window = jnp.arange(experts, dtype=jnp.int32)
    hits = expert_ids[..., None] == window
    member = jnp.any(hits, axis=-2).astype(jnp.int32)
    weight = jnp.sum(jnp.where(hits, gates[..., None], jnp.float32(0.0)), axis=-2)
    rank = jnp.cumsum(member, axis=-2) - member
    slots = jnp.arange(capacity, dtype=jnp.int32)
    place = (member[..., None] == 1) & (rank[..., None] == slots)
    return (place, weight)


def per_device(tokens, expert_ids, gate_codes, w_gate, w_up, w_down):
    experts = lax.axis_size(EXPERT)
    gathered = gathered_copies(tokens, "group", 1)
    place, weight = routing(expert_ids[0], gate_codes[0], experts, CAPG)
    pick = place.astype(jnp.bfloat16)
    rows = jnp.einsum("tej,td->ejd", pick, gathered[0], preferred_element_type=jnp.float32).astype(
        jnp.bfloat16
    )
    mix = jnp.where(place, weight[..., None], jnp.float32(0.0))
    slot_rows = lax.all_to_all(rows, EXPERT, split_axis=0, concat_axis=0, tiled=True)
    count = slot_rows.shape[0] * slot_rows.shape[1]
    flat = slot_rows.reshape(count, slot_rows.shape[2])
    first = jnp.dot(flat, w_gate[0], preferred_element_type=jnp.float32)
    second = jnp.dot(flat, w_up[0], preferred_element_type=jnp.float32)
    hidden = (jax.nn.silu(first) * second).astype(jnp.bfloat16)
    partial_value = jnp.dot(hidden, w_down[0], preferred_element_type=jnp.float32).astype(
        jnp.bfloat16
    )
    partial_value = partial_value.reshape(slot_rows.shape)
    returned = core_and_chips(partial_value, ("expert_0", "expert_1"), (1, 0), 0, 0)
    mixed = sent_and_summed(
        jnp.einsum(
            "tej,ejd->td",
            mix,
            returned,
            precision=lax.Precision.HIGHEST,
            preferred_element_type=jnp.float32,
        ),
        "group",
        0,
    ).astype(jnp.bfloat16)
    return mixed[None]


def solution(mesh):
    torus = Mesh(
        mesh.devices.reshape(mesh.shape["group"], 16, 2, mesh.shape["dp"]),
        ("group", "expert_0", "expert_1", "dp"),
    )
    placed = (
        P(EXPERT_DP, "group", None),
        P(EXPERT_DP, None, None),
        P(EXPERT_DP, None, None),
        P(EXPERT, None, "group"),
        P(EXPERT, None, "group"),
        P(EXPERT, "group", None),
    )
    return jax.shard_map(
        per_device,
        mesh=torus,
        in_specs=placed,
        out_specs=P(EXPERT_DP, "group", None),
        check_vma=False,
    )
```

profile of v0, /device:TPU:64, one launch (start us, length us, event | category | flops | bytes accessed | tf_op | source)
XLA Modules:
  0.0 322.5 jit_solution(15766459316250367731)
XLA Ops:
  0.0 0.0 copy-start
  0.0 0.0 copy-start.2
  0.0 2.2 broadcast_in_dim.48
  2.2 9.7 %all-to-all-start = ((bf16[16,1,4,7168]{3,2,1,0:T(4,128)(2,1)}), bf16[16,1,4,7168]{3,2,1,0:T(4,128)(2,1)}, u32[]{:S(2)}, u32[]{:S(2)}) async-start(bf16[16,1,4,7168]{3,2,1,0:T(4,128)(2,1)} %broadcast_in_dim.48), calls=%async_computation | async-start | bytes 1835008 | tf_op jit(solution)/shard_map/all_to_all | solution.py:14
  11.9 0.0 copy-done.2
  11.9 1.8 copy.52
  13.8 1.3 fusion.36
  15.1 0.6 copy.56
  15.7 23.6 %all-to-all-done = bf16[16,1,4,7168]{3,2,1,0:T(4,128)(2,1)} async-done(((bf16[16,1,4,7168]{3,2,1,0:T(4,128)(2,1)}), bf16[16,1,4,7168]{3,2,1,0:T(4,128)(2,1)}, u32[]{:S(2)}, u32[]{:S(2)}) %all-to-all-start) | async-done | bytes 917536 | tf_op jit(solution)/shard_map/all_to_all | solution.py:14
  39.3 2.4 reshape.76
  41.6 1.8 convolution_convert_fusion.1
  43.5 1.4 copy.57
  44.9 106.8 %all_to_all.25 = bf16[32,4,7168]{2,1,0:T(4,128)(2,1)} all-to-all(bf16[32,4,7168]{2,1,0:T(4,128)(2,1)S(1)} %copy.57), channel_id=1, replica_groups=mesh['group'=16,'expert_0'=16,'expert_1'=2,'dp'=2] {'expert_0','expert_1'}, dimensions={0} | all-to-all | bytes 3670016 | tf_op jit(solution)/shard_map/all_to_all | solution.py:78
  151.7 4.0 %reshape.73 = bf16[128,7168]{1,0:T(8,128)(2,1)} reshape(bf16[32,4,7168]{2,1,0:T(4,128)(2,1)} %all_to_all.25) | data formatting | bytes 3670016 | tf_op jit(solution)/shard_map/reshape | solution.py:80
  155.6 2.7 fusion.5
  158.3 0.0 copy-done
  158.3 4.5 %convolution_convert_fusion = bf16[128,7168]{1,0:T(8,128)(2,1)} fusion(bf16[1,128,7168]{2,1,0:T(8,128)(2,1)S(1)} %copy-done, bf16[128,7168]{1,0:T(8,128)(2,1)} %reshape.73, bf16[1,7168,128]{2,1,0:T(8,128)(2,1)} %param.10, f32[128,128]{1,0:T(8,128)S(1)} %fusion.5), kind=kOutput, calls=%fused_computation | convolution fusion | flops 470777856 | bytes 7405568 | tf_op jit(solution)/shard_map/dot_general | solution.py:84
  162.8 4.1 %reshape_reshape_reshape.3 = bf16[16,2,1,4,7168]{4,3,1,0,2:T(4,128)(2,1)} reshape(bf16[128,7168]{1,0:T(8,128)(2,1)} %convolution_convert_fusion) | data formatting | bytes 3670016 | tf_op jit(solution)/shard_map/reshape;reshape;reshape | solution.py:38
  166.9 2.1 copy.58
  169.1 5.2 %all_to_all.26 = bf16[16,2,1,4,7168]{4,3,0,2,1:T(4,128)(2,1)S(1)} all-to-all(bf16[16,2,1,4,7168]{4,3,0,2,1:T(4,128)(2,1)S(1)} %copy.58), channel_id=1, replica_groups=mesh['group'=16,'expert_0'=16,'expert_1'=2,'dp'=2] {'expert_1'}, dimensions={1} | all-to-all | bytes 3670016 | tf_op jit(solution)/shard_map/all_to_all | solution.py:40
  174.3 2.1 copy.59
  176.4 0.0 copy-start.1
  176.4 6.1 %all-to-all-start.3 = ((bf16[16,2,1,4,7168]{4,3,1,2,0:T(4,128)(2,1)}), bf16[16,2,1,4,7168]{4,3,1,2,0:T(4,128)(2,1)}, u32[]{:S(2)}, u32[]{:S(2)}) async-start(bf16[16,2,1,4,7168]{4,3,1,2,0:T(4,128)(2,1)} %copy.59), calls=%async_computation.3 | async-start | bytes 3670016 | tf_op jit(solution)/shard_map/all_to_all | solution.py:40
  182.4 0.0 copy-done.1
  182.5 0.1 copy.54
  182.6 0.1 copy.50
  182.7 1.1 reduce.1
  183.9 83.0 %all-to-all-done.3 = bf16[16,2,1,4,7168]{4,3,1,2,0:T(4,128)(2,1)} async-done(((bf16[16,2,1,4,7168]{4,3,1,2,0:T(4,128)(2,1)}), bf16[16,2,1,4,7168]{4,3,1,2,0:T(4,128)(2,1)}, u32[]{:S(2)}, u32[]{:S(2)}) %all-to-all-start.3) | async-done | bytes 1835040 | tf_op jit(solution)/shard_map/all_to_all | solution.py:40
  266.9 3.3 %convolution_bitcast_fusion = f32[16,4,7168]{2,0,1:T(8,128)S(1)} fusion(bf16[32,4,7168]{2,1,0:T(4,128)(2,1)} %bitcast.10, f32[16,4,32]{2,0,1:T(8,128)S(1)} %copy.55, s32[16,4,32]{2,0,1:T(8,128)S(1)} %copy.53, pred[16,4,32]{2,0,1:T(8,128)(4,1)S(1)} %copy.51), kind=kOutput, calls=%fused_computation.2 | convolution fusion | flops 704667648 | bytes 3688448 | tf_op jit(solution)/shard_map/tej,ejd->td/dot_general | solution.py:90
  270.2 1.2 copy.61
  271.4 48.7 %all_to_all.27 = f32[16,4,7168]{2,1,0:T(4,128)} all-to-all(f32[16,4,7168]{2,1,0:T(4,128)S(1)} %copy.61), channel_id=1, replica_groups=mesh['group'=16,'expert_0'=16,'expert_1'=2,'dp'=2] {'group'}, dimensions={0} | all-to-all | bytes 3670016 | tf_op jit(solution)/shard_map/all_to_all | solution.py:52
  320.1 2.4 reduce_sum.29
  (11 shorter events, 0.1 us)
Async XLA Ops:
  0.0 158.3 %copy-start = (bf16[1,128,7168]{2,1,0:T(8,128)(2,1)S(1)}, bf16[1,128,7168]{2,1,0:T(8,128)(2,1)}, u32[]{:S(2)}) copy-start(bf16[1,128,7168]{2,1,0:T(8,128)(2,1)} %param.11) | copy-start | bytes 5505028
  0.0 11.9 %copy-start.2 = (s32[1,64,8]{1,2,0:T(8,128)S(1)}, s32[1,64,8]{1,2,0:T(8,128)}, u32[]{:S(2)}) copy-start(s32[1,64,8]{1,2,0:T(8,128)} %param.7) | copy-start | bytes 6148
  2.2 37.1 %all-to-all-start = ((bf16[16,1,4,7168]{3,2,1,0:T(4,128)(2,1)}), bf16[16,1,4,7168]{3,2,1,0:T(4,128)(2,1)}, u32[]{:S(2)}, u32[]{:S(2)}) async-start(bf16[16,1,4,7168]{3,2,1,0:T(4,128)(2,1)} %broadcast_in_dim.48), calls=%async_computation | async-start | bytes 1835008 | tf_op jit(solution)/shard_map/all_to_all | solution.py:14
  176.4 6.1 %copy-start.1 = (s32[1,64,8]{1,2,0:T(8,128)S(1)}, s32[1,64,8]{1,2,0:T(8,128)}, u32[]{:S(2)}) copy-start(s32[1,64,8]{1,2,0:T(8,128)} %param.8) | copy-start | bytes 6148
  176.4 90.5 %all-to-all-start.3 = ((bf16[16,2,1,4,7168]{4,3,1,2,0:T(4,128)(2,1)}), bf16[16,2,1,4,7168]{4,3,1,2,0:T(4,128)(2,1)}, u32[]{:S(2)}, u32[]{:S(2)}) async-start(bf16[16,2,1,4,7168]{4,3,1,2,0:T(4,128)(2,1)} %copy.59), calls=%async_computation.3 | async-start | bytes 3670016 | tf_op jit(solution)/shard_map/all_to_all | solution.py:40
where the time goes:
time: 323 us; the launch traced here: 322 us
  blocking collectives  161 us (50%)
  waiting for transfers between devices  107 us (33%)
  local copies, waits for them, and re-layouts  22.1 us (7%)
  starting transfers between devices  15.8 us (5%)
  matrix products  12.3 us (4%)
  other arithmetic  5.01 us (2%)
    all_to_all x1, blocking collectives, per_device(): lax.all_to_all(rows, EXPERT, split_axis=0, concat_axis=0, tiled=True)  107 us
    all_to_all x1, waiting for transfers between devices, turned_blocks(): whole = lax.all_to_all(whole, axes[k], k, k, tiled=True)  83 us
    all_to_all x1, blocking collectives, sent_and_summed(): lax.all_to_all(in_blocks(shard, dim, length), axis, 0, 0, tiled=True)  48.7 us
    all_to_all x1, waiting for transfers between devices, sent_to_all(): lax.all_to_all(jnp.broadcast_to(shard[None], (length, *shard.shape)), axi...  23.6 us
    all_to_all x1, starting transfers between devices, sent_to_all(): lax.all_to_all(jnp.broadcast_to(shard[None], (length, *shard.shape)), axi...  9.71 us
  transfers between devices with their start and end apart: 2, of which 2 were waited for; matrix products, arithmetic and copies ran while one was open for 2% of the time, Pallas kernels for 0%

commit v1 on v0

v1 whole, which is shorter than its diff:
```python
import jax
import jax.numpy as jnp
from jax import lax
from jax.sharding import Mesh
from jax.sharding import PartitionSpec as P


CAPG = 4
GROUP = ("y", "xh")
EXPERT = ("z", "core")
SETS_OVER = ("z", "core", "dp")


def exchange(parts, axes):
    return lax.all_to_all(parts, axes, 0, 0, tiled=True)


def in_columns(rows, pieces):
    cols = rows.shape[1] // pieces
    return jnp.stack([rows[:, i * cols : (i + 1) * cols] for i in range(pieces)])


def routing(expert_ids, gate_codes, experts, capacity):
    window = jnp.arange(experts, dtype=jnp.int32)
    hits = expert_ids[..., None] == window
    member = jnp.any(hits, axis=-2)
    codes = gate_codes.astype(jnp.float32)
    gates = 2.5 * codes / jnp.sum(codes, axis=-1, keepdims=True)
    weight = jnp.sum(jnp.where(hits, gates[..., None], jnp.float32(0.0)), axis=-2)
    tokens = expert_ids.shape[0]
    before = jnp.tril(jnp.ones((tokens, tokens), jnp.bfloat16), -1)
    rank = jnp.dot(before, member.astype(jnp.bfloat16), preferred_element_type=jnp.float32)
    slots = jnp.arange(capacity, dtype=jnp.float32)
    place = member[..., None] & (rank[..., None] == slots)
    return place, weight


def around(shard, axis):
    n = lax.axis_size(axis)
    up = [(i, (i + 1) % n) for i in range(n)]
    down = [(i, (i - 1) % n) for i in range(n)]
    found = [(0, shard)]
    a = b = shard
    for k in range(1, n // 2 + 1):
        a = lax.ppermute(a, axis, up)
        found.append((-k, a))
        if 2 * k < n:
            b = lax.ppermute(b, axis, down)
            found.append((k, b))
    return found


def per_device(tokens, expert_ids, gate_codes, w_gate, w_up, w_down):
    ny, nh = lax.axis_size("y"), lax.axis_size("xh")
    experts = lax.axis_size(EXPERT)
    own, width = tokens.shape[1], tokens.shape[2]
    cols = width // ny
    hid = w_gate.shape[2]
    here = lax.axis_index("y")

    blocks = in_columns(tokens[0], ny)
    blocks = jnp.broadcast_to(blocks[:, None], (ny, nh, own, cols))
    toks = exchange(blocks.reshape(ny * nh, own, cols), GROUP)
    blocks = [w_down[0][:, i * cols : (i + 1) * cols] for i in range(ny)]
    blocks = jnp.stack(blocks)
    downs = {}
    for k in sorted(range(1, ny), key=lambda k: -min(k, ny - k)):
        block = lax.dynamic_index_in_dim(blocks, lax.rem(here + k, ny), 0, keepdims=False)
        downs[k] = lax.ppermute(block, "y", [(i, (i + k) % ny) for i in range(ny)])
    downs[0] = lax.dynamic_index_in_dim(blocks, here, 0, keepdims=False)

    place, weight = routing(expert_ids[0], gate_codes[0], experts, CAPG)
    mix = jnp.where(place, weight[..., None], jnp.float32(0.0))
    rows = jnp.einsum(
        "tej,td->ejd",
        place.astype(jnp.bfloat16),
        toks.reshape(ny * nh * own, cols),
        preferred_element_type=jnp.float32,
    ).astype(jnp.bfloat16)
    got = exchange(rows, EXPERT)
    sets = got.shape[0]
    count = sets * CAPG
    gate_blocks = w_gate[0].reshape(ny, cols, hid)
    up_blocks = w_up[0].reshape(ny, cols, hid)
    first = second = jnp.float32(0.0)
    for step, shard in around(got.reshape(count, cols), "y"):
        at = lax.rem(here + step + ny, ny)
        gate = lax.dynamic_index_in_dim(gate_blocks, at, 0, keepdims=False)
        up = lax.dynamic_index_in_dim(up_blocks, at, 0, keepdims=False)
        first += jnp.dot(shard, gate, preferred_element_type=jnp.float32)
        second += jnp.dot(shard, up, preferred_element_type=jnp.float32)
    hidden = (jax.nn.silu(first) * second).astype(jnp.bfloat16)
    hiddens = exchange(jnp.broadcast_to(hidden[None], (ny, count, hid)), "y")
    outs = jnp.float32(0.0)
    for k in range(ny):
        part = lax.dynamic_index_in_dim(hiddens, lax.rem(here - k + ny, ny), 0, keepdims=False)
        outs += jnp.dot(part, downs[k], preferred_element_type=jnp.float32)
    outs = outs.astype(jnp.bfloat16)
    back = exchange(outs.reshape(sets, CAPG, cols), EXPERT)
    mixed = jnp.einsum(
        "tej,ejc->tc",
        mix,
        back.astype(jnp.float32),
        precision=lax.Precision.HIGHEST,
        preferred_element_type=jnp.float32,
    )
    home = exchange(mixed.astype(jnp.bfloat16).reshape(ny * nh, own, cols), GROUP)
    home = home.reshape(ny, nh, own, cols).astype(jnp.float32)
    home = jnp.sum(home, axis=1).astype(jnp.bfloat16)
    return jnp.concatenate([home[i] for i in range(ny)], axis=1)[None]


def solution(mesh):
    fine = Mesh(
        mesh.devices.reshape(8, 2, 16, 2, mesh.shape["dp"]), ("y", "xh", "z", "core", "dp")
    )
    placed = (
        P(SETS_OVER, GROUP, None),
        P(SETS_OVER, None, None),
        P(SETS_OVER, None, None),
        P(EXPERT, None, GROUP),
        P(EXPERT, None, GROUP),
        P(EXPERT, GROUP, None),
    )
    return jax.shard_map(
        per_device,
        mesh=fine,
        in_specs=placed,
        out_specs=P(SETS_OVER, GROUP, None),
        check_vma=False,
    )
```

time: 323 us -> 219 us (0.68)
  the two profiles are of different devices: /device:TPU:64 before, /device:TPU:2 now
where the time goes in v1:
time: 219 us; the launch traced here: 217 us
  starting transfers between devices  91.1 us (42%)
  waiting for transfers between devices  68.6 us (31%)
  local copies, waits for them, and re-layouts  25.2 us (12%)
  blocking collectives  17.4 us (8%)
  matrix products  13.6 us (6%)
    all_to_all x4, waiting for transfers between devices, exchange(): return lax.all_to_all(parts, axes, 0, 0, tiled=True)  41.2 us
    all_to_all x4, starting transfers between devices, exchange(): return lax.all_to_all(parts, axes, 0, 0, tiled=True)  38.2 us
    ppermute x7, starting transfers between devices, per_device(): downs[k] = lax.ppermute(block, 'y', [(i, (i + k) % ny) for i in range(ny)])  29.2 us
    all_to_all x1, blocking collectives, exchange(): return lax.all_to_all(parts, axes, 0, 0, tiled=True)  17.4 us
    unnamed x31, local copies, waits for them, and re-layouts  17.3 us
    ppermute x3, starting transfers between devices, around(): b = lax.ppermute(b, axis, down)  15.6 us
    ppermute x4, waiting for transfers between devices, around(): a = lax.ppermute(a, axis, up)  12.4 us
    ppermute x7, waiting for transfers between devices, per_device(): downs[k] = lax.ppermute(block, 'y', [(i, (i + k) % ny) for i in range(ny)])  11.8 us
  transfers between devices with their start and end apart: 18, of which 10 were waited for; matrix products, arithmetic and copies ran while one was open for 13% of the time, Pallas kernels for 0%

profile of v1, /device:TPU:2, one launch (start us, length us, event | category | flops | bytes accessed | tf_op | source)
XLA Modules:
  0.0 217.2 jit_solution(15659771201314144851)
XLA Ops:
  0.0 0.8 constant_dynamic-update-slice_fusion.7
  6.5 8.8 %all-to-all-start = ((bf16[16,4,896]{2,1,0:T(4,128)(2,1)}), bf16[16,4,896]{2,1,0:T(4,128)(2,1)S(1)}, u32[]{:S(2)}, u32[]{:S(2)}) async-start(bf16[16,4,896]{2,1,0:T(4,128)(2,1)} %bitcast.11), calls=%async_computation | async-start | bytes 229376 | tf_op jit(solution)/shard_map/all_to_all | solution.py:15
  16.0 1.7 fusion.18
  17.7 1.6 fusion.17
  19.3 1.6 fusion.16
  21.1 5.1 %all-to-all-done = bf16[16,4,896]{2,1,0:T(4,128)(2,1)S(1)} async-done(((bf16[16,4,896]{2,1,0:T(4,128)(2,1)}), bf16[16,4,896]{2,1,0:T(4,128)(2,1)S(1)}, u32[]{:S(2)}, u32[]{:S(2)}) %all-to-all-start) | async-done | bytes 114720 | tf_op jit(solution)/shard_map/all_to_all | solution.py:15
  26.4 0.8 copy.18
  27.3 19.2 %all-to-all-start.1 = ((bf16[32,4,896]{2,1,0:T(4,128)(2,1)}), bf16[32,4,896]{2,1,0:T(4,128)(2,1)S(1)}, u32[]{:S(2)}, u32[]{:S(2)}) async-start(bf16[32,4,896]{2,1,0:T(4,128)(2,1)} %copy.18), calls=%async_computation.1 | async-start | bytes 458752 | tf_op jit(solution)/shard_map/all_to_all | solution.py:15
  46.4 1.6 fusion.15
  48.1 1.7 fusion.14
  49.7 1.7 fusion.13
  51.4 1.6 fusion.12
  53.0 14.8 %all-to-all-done.1 = bf16[32,4,896]{2,1,0:T(4,128)(2,1)S(1)} async-done(((bf16[32,4,896]{2,1,0:T(4,128)(2,1)}), bf16[32,4,896]{2,1,0:T(4,128)(2,1)S(1)}, u32[]{:S(2)}, u32[]{:S(2)}) %all-to-all-start.1) | async-done | bytes 229408 | tf_op jit(solution)/shard_map/all_to_all | solution.py:15
  67.9 2.5 %collective-permute-start = (bf16[128,896]{1,0:T(8,128)(2,1)S(1)}, bf16[128,896]{1,0:T(8,128)(2,1)S(1)}, u32[]{:S(2)}, u32[]{:S(2)}) collective-permute-start(bf16[128,896]{1,0:T(8,128)(2,1)S(1)} %reshape.51), channel_id=1, source_target_pairs={{0,128},{128,256},{256,384},{384,512},{512,640},{640,768},{768,896... | collective-permute-start | bytes 688136 | tf_op jit(solution)/shard_map/ppermute | solution.py:45
  70.4 4.7 %collective-permute-start.1 = (bf16[128,896]{1,0:T(8,128)(2,1)S(1)}, bf16[128,896]{1,0:T(8,128)(2,1)S(1)}, u32[]{:S(2)}, u32[]{:S(2)}) collective-permute-start(bf16[128,896]{1,0:T(8,128)(2,1)S(1)} %reshape.51), channel_id=1, source_target_pairs={{0,896},{128,0},{256,128},{384,256},{512,384},{640,512},{768,640},... | collective-permute-start | bytes 688136 | tf_op jit(solution)/shard_map/ppermute | solution.py:48
  75.3 1.2 fusion.30
  76.5 2.5 %collective-permute-done.1 = bf16[128,896]{1,0:T(8,128)(2,1)S(1)} collective-permute-done((bf16[128,896]{1,0:T(8,128)(2,1)S(1)}, bf16[128,896]{1,0:T(8,128)(2,1)S(1)}, u32[]{:S(2)}, u32[]{:S(2)}) %collective-permute-start.1) | collective-permute-done | bytes 229408 | tf_op jit(solution)/shard_map/ppermute | solution.py:48
  79.0 5.6 %collective-permute-start.3 = (bf16[128,896]{1,0:T(8,128)(2,1)S(1)}, bf16[128,896]{1,0:T(8,128)(2,1)S(1)}, u32[]{:S(2)}, u32[]{:S(2)}) collective-permute-start(bf16[128,896]{1,0:T(8,128)(2,1)S(1)} %collective-permute-done.1), channel_id=1, source_target_pairs={{0,896},{128,0},{256,128},{384,256},{512,384},{640,512},{768,640},... | collective-permute-start | bytes 688136 | tf_op jit(solution)/shard_map/ppermute | solution.py:48
  84.6 1.9 collective-permute-start.2
  86.8 1.2 convolution_add_fusion.6
  88.4 5.3 %collective-permute-start.5 = (bf16[128,896]{1,0:T(8,128)(2,1)S(1)}, bf16[128,896]{1,0:T(8,128)(2,1)S(1)}, u32[]{:S(2)}, u32[]{:S(2)}) collective-permute-start(bf16[128,896]{1,0:T(8,128)(2,1)S(1)} %collective-permute-done.3), channel_id=1, source_target_pairs={{0,896},{128,0},{256,128},{384,256},{512,384},{640,512},{768,640},... | collective-permute-start | bytes 688136 | tf_op jit(solution)/shard_map/ppermute | solution.py:48
  94.2 1.9 collective-permute-start.4
  97.7 5.6 %collective-permute-done.4 = bf16[128,896]{1,0:T(8,128)(2,1)S(1)} collective-permute-done((bf16[128,896]{1,0:T(8,128)(2,1)S(1)}, bf16[128,896]{1,0:T(8,128)(2,1)S(1)}, u32[]{:S(2)}, u32[]{:S(2)}) %collective-permute-start.4) | collective-permute-done | bytes 229408 | tf_op jit(solution)/shard_map/ppermute | solution.py:45
  103.3 1.9 collective-permute-start.6
  105.7 6.7 %collective-permute-done.6 = bf16[128,896]{1,0:T(8,128)(2,1)S(1)} collective-permute-done((bf16[128,896]{1,0:T(8,128)(2,1)S(1)}, bf16[128,896]{1,0:T(8,128)(2,1)S(1)}, u32[]{:S(2)}, u32[]{:S(2)}) %collective-permute-start.6) | collective-permute-done | bytes 229408 | tf_op jit(solution)/shard_map/ppermute | solution.py:45
  112.9 0.8 broadcast_in_dim.60
  113.7 3.4 %all-to-all-start.2 = ((bf16[8,128,128]{2,1,0:T(8,128)(2,1)}), bf16[8,128,128]{2,1,0:T(8,128)(2,1)S(1)}, u32[]{:S(2)}, u32[]{:S(2)}) async-start(bf16[8,128,128]{2,1,0:T(8,128)(2,1)} %broadcast_in_dim.60), calls=%async_computation.2 | async-start | bytes 524288 | tf_op jit(solution)/shard_map/all_to_all | solution.py:15
  117.1 1.6 fusion.11
  118.7 2.3 %dynamic-slice_bitcast_fusion.5 = (bf16[128,896]{1,0:T(8,128)(2,1)S(1)}, bf16[128,896]{1,0:T(8,128)(2,1)S(1)}, bf16[128,896]{1,0:T(8,128)(2,1)S(1)}, bf16[128,89...) fusion(bf16[8,128,896]{2,1,0:T(8,128)(2,1)} %fusion.11, ...), kind=kLoop, calls=%fused_computation.71 | loop fusion | bytes 3211292 | tf_op jit(solution)/shard_map/jit(dynamic_index_in_dim)/squeeze | solution.py:68
  121.1 3.8 %collective-permute-start.7 = (bf16[128,896]{1,0:T(8,128)(2,1)}, bf16[128,896]{1,0:T(8,128)(2,1)}, u32[]{:S(2)}, u32[]{:S(2)}) collective-permute-start(bf16[128,896]{1,0:T(8,128)(2,1)} %get-tuple-element.11), channel_id=1, source_target_pairs={{0,128},{128,256},{256,384},{384,512},{512,640},{640,768},{768,896... | collective-permute-start | bytes 688136 | tf_op jit(solution)/shard_map/ppermute | solution.py:69
  124.9 6.4 %collective-permute-start.9 = (bf16[128,896]{1,0:T(8,128)(2,1)S(1)}, bf16[128,896]{1,0:T(8,128)(2,1)}, u32[]{:S(2)}, u32[]{:S(2)}) collective-permute-start(bf16[128,896]{1,0:T(8,128)(2,1)S(1)} %get-tuple-element.10), channel_id=1, source_target_pairs={{0,384},{128,512},{256,640},{384,768},{512,896},{640,0},{768,128},... | collective-permute-start | bytes 688136 | tf_op jit(solution)/shard_map/ppermute | solution.py:69
  131.3 2.0 collective-permute-start.10
  133.3 6.9 %collective-permute-start.11 = (bf16[128,896]{1,0:T(8,128)(2,1)S(1)}, bf16[128,896]{1,0:T(8,128)(2,1)}, u32[]{:S(2)}, u32[]{:S(2)}) collective-permute-start(bf16[128,896]{1,0:T(8,128)(2,1)S(1)} %get-tuple-element.8), channel_id=1, source_target_pairs={{0,640},{128,768},{256,896},{384,0},{512,128},{640,256},{768,384},... | collective-permute-start | bytes 688136 | tf_op jit(solution)/shard_map/ppermute | solution.py:69
  140.2 3.4 %collective-permute-start.12 = (bf16[128,896]{1,0:T(8,128)(2,1)S(1)}, bf16[128,896]{1,0:T(8,128)(2,1)}, u32[]{:S(2)}, u32[]{:S(2)}) collective-permute-start(bf16[128,896]{1,0:T(8,128)(2,1)S(1)} %get-tuple-element.7), channel_id=1, source_target_pairs={{0,768},{128,896},{256,0},{384,128},{512,256},{640,384},{768,512},... | collective-permute-start | bytes 688136 | tf_op jit(solution)/shard_map/ppermute | solution.py:69
  143.5 1.2 fusion.19
  144.7 2.5 %collective-permute-start.13 = (bf16[128,896]{1,0:T(8,128)(2,1)S(1)}, bf16[128,896]{1,0:T(8,128)(2,1)S(1)}, u32[]{:S(2)}, u32[]{:S(2)}) collective-permute-start(bf16[128,896]{1,0:T(8,128)(2,1)S(1)} %get-tuple-element.6), channel_id=1, source_target_pairs={{0,896},{128,0},{256,128},{384,256},{512,384},{640,512},{768,640},... | collective-permute-start | bytes 688136 | tf_op jit(solution)/shard_map/ppermute | solution.py:69
  147.2 1.2 convolution_add_fusion.1
  148.4 4.3 %collective-permute-start.8 = (bf16[128,896]{1,0:T(8,128)(2,1)S(1)}, bf16[128,896]{1,0:T(8,128)(2,1)S(1)}, u32[]{:S(2)}, u32[]{:S(2)}) collective-permute-start(bf16[128,896]{1,0:T(8,128)(2,1)S(1)} %get-tuple-element.5), channel_id=1, source_target_pairs={{0,256},{128,384},{256,512},{384,640},{512,768},{640,896},{768,0},... | collective-permute-start | bytes 688136 | tf_op jit(solution)/shard_map/ppermute | solution.py:69
  152.6 1.2 fusion.74
  153.8 7.9 %collective-permute-done.10 = bf16[128,896]{1,0:T(8,128)(2,1)} collective-permute-done((bf16[128,896]{1,0:T(8,128)(2,1)S(1)}, bf16[128,896]{1,0:T(8,128)(2,1)}, u32[]{:S(2)}, u32[]{:S(2)}) %collective-permute-start.10) | collective-permute-done | bytes 229408 | tf_op jit(solution)/shard_map/ppermute | solution.py:69
  161.7 1.1 fusion.72
  162.8 1.6 collective-permute-done.11
  164.4 1.1 fusion.70
  165.6 1.2 fusion.68
  166.8 2.4 %collective-permute-done.13 = bf16[128,896]{1,0:T(8,128)(2,1)S(1)} collective-permute-done((bf16[128,896]{1,0:T(8,128)(2,1)S(1)}, bf16[128,896]{1,0:T(8,128)(2,1)S(1)}, u32[]{:S(2)}, u32[]{:S(2)}) %collective-permute-start.13) | collective-permute-done | bytes 229408 | tf_op jit(solution)/shard_map/ppermute | solution.py:69
  170.4 6.8 %all-to-all-start.3 = ((bf16[32,4,896]{2,1,0:T(4,128)(2,1)}), bf16[32,4,896]{2,1,0:T(4,128)(2,1)S(1)}, u32[]{:S(2)}, u32[]{:S(2)}) async-start(bf16[32,4,896]{2,1,0:T(4,128)(2,1)} %reshape.52), calls=%async_computation.3 | async-start | bytes 458752 | tf_op jit(solution)/shard_map/all_to_all | solution.py:15
  177.3 21.3 %all-to-all-done.3 = bf16[32,4,896]{2,1,0:T(4,128)(2,1)S(1)} async-done(((bf16[32,4,896]{2,1,0:T(4,128)(2,1)}), bf16[32,4,896]{2,1,0:T(4,128)(2,1)S(1)}, u32[]{:S(2)}, u32[]{:S(2)}) %all-to-all-start.3) | async-done | bytes 229408 | tf_op jit(solution)/shard_map/all_to_all | solution.py:15
  199.0 17.4 %all_to_all.25 = bf16[16,4,896]{2,1,0:T(4,128)(2,1)S(1)} all-to-all(bf16[16,4,896]{2,1,0:T(4,128)(2,1)S(1)} %reshape.53), channel_id=1, replica_groups=mesh['y'=8,'xh'=2,'z'=16,'core'=2,'dp'=2] {'y','xh'}, dimensions={0} | all-to-all | bytes 229376 | tf_op jit(solution)/shard_map/all_to_all | solution.py:15
  (64 shorter events, 13.0 us)
Async XLA Ops:
  0.0 75.1 %copy-start = (bf16[1,7168,128]{2,1,0:T(8,128)(2,1)S(1)}, bf16[1,7168,128]{2,1,0:T(8,128)(2,1)}, u32[]{:S(2)}) copy-start(bf16[1,7168,128]{2,1,0:T(8,128)(2,1)} %param.9) | copy-start | bytes 5505028
  6.5 19.8 %all-to-all-start = ((bf16[16,4,896]{2,1,0:T(4,128)(2,1)}), bf16[16,4,896]{2,1,0:T(4,128)(2,1)S(1)}, u32[]{:S(2)}, u32[]{:S(2)}) async-start(bf16[16,4,896]{2,1,0:T(4,128)(2,1)} %bitcast.11), calls=%async_computation | async-start | bytes 229376 | tf_op jit(solution)/shard_map/all_to_all | solution.py:15
  27.3 40.6 %all-to-all-start.1 = ((bf16[32,4,896]{2,1,0:T(4,128)(2,1)}), bf16[32,4,896]{2,1,0:T(4,128)(2,1)S(1)}, u32[]{:S(2)}, u32[]{:S(2)}) async-start(bf16[32,4,896]{2,1,0:T(4,128)(2,1)} %copy.18), calls=%async_computation.1 | async-start | bytes 458752 | tf_op jit(solution)/shard_map/all_to_all | solution.py:15
  67.9 20.3 %copy-start.1 = (bf16[1,7168,128]{2,1,0:T(8,128)(2,1)S(1)}, bf16[1,7168,128]{2,1,0:T(8,128)(2,1)}, u32[]{:S(2)}) copy-start(bf16[1,7168,128]{2,1,0:T(8,128)(2,1)} %param.10) | copy-start | bytes 5505028
  67.9 16.7 %collective-permute-start = (bf16[128,896]{1,0:T(8,128)(2,1)S(1)}, bf16[128,896]{1,0:T(8,128)(2,1)S(1)}, u32[]{:S(2)}, u32[]{:S(2)}) collective-permute-start(bf16[128,896]{1,0:T(8,128)(2,1)S(1)} %reshape.51), channel_id=1, source_target_pairs={{0,128},{128,256},{256,384},{384,512},{512,640},{640,768},{768,896... | collective-permute-start | bytes 688136 | tf_op jit(solution)/shard_map/ppermute | solution.py:45
  70.4 8.6 %collective-permute-start.1 = (bf16[128,896]{1,0:T(8,128)(2,1)S(1)}, bf16[128,896]{1,0:T(8,128)(2,1)S(1)}, u32[]{:S(2)}, u32[]{:S(2)}) collective-permute-start(bf16[128,896]{1,0:T(8,128)(2,1)S(1)} %reshape.51), channel_id=1, source_target_pairs={{0,896},{128,0},{256,128},{384,256},{512,384},{640,512},{768,640},... | collective-permute-start | bytes 688136 | tf_op jit(solution)/shard_map/ppermute | solution.py:48
  79.0 9.4 %collective-permute-start.3 = (bf16[128,896]{1,0:T(8,128)(2,1)S(1)}, bf16[128,896]{1,0:T(8,128)(2,1)S(1)}, u32[]{:S(2)}, u32[]{:S(2)}) collective-permute-start(bf16[128,896]{1,0:T(8,128)(2,1)S(1)} %collective-permute-done.1), channel_id=1, source_target_pairs={{0,896},{128,0},{256,128},{384,256},{512,384},{640,512},{768,640},... | collective-permute-start | bytes 688136 | tf_op jit(solution)/shard_map/ppermute | solution.py:48
  84.6 9.6 %collective-permute-start.2 = (bf16[128,896]{1,0:T(8,128)(2,1)S(1)}, bf16[128,896]{1,0:T(8,128)(2,1)S(1)}, u32[]{:S(2)}, u32[]{:S(2)}) collective-permute-start(bf16[128,896]{1,0:T(8,128)(2,1)S(1)} %collective-permute-done), channel_id=1, source_target_pairs={{0,128},{128,256},{256,384},{384,512},{512,640},{640,768},{768,896... | collective-permute-start | bytes 688136 | tf_op jit(solution)/shard_map/ppermute | solution.py:45
  88.4 8.8 %collective-permute-start.5 = (bf16[128,896]{1,0:T(8,128)(2,1)S(1)}, bf16[128,896]{1,0:T(8,128)(2,1)S(1)}, u32[]{:S(2)}, u32[]{:S(2)}) collective-permute-start(bf16[128,896]{1,0:T(8,128)(2,1)S(1)} %collective-permute-done.3), channel_id=1, source_target_pairs={{0,896},{128,0},{256,128},{384,256},{512,384},{640,512},{768,640},... | collective-permute-start | bytes 688136 | tf_op jit(solution)/shard_map/ppermute | solution.py:48
  94.2 9.1 %collective-permute-start.4 = (bf16[128,896]{1,0:T(8,128)(2,1)S(1)}, bf16[128,896]{1,0:T(8,128)(2,1)S(1)}, u32[]{:S(2)}, u32[]{:S(2)}) collective-permute-start(bf16[128,896]{1,0:T(8,128)(2,1)S(1)} %collective-permute-done.2), channel_id=1, source_target_pairs={{0,128},{128,256},{256,384},{384,512},{512,640},{640,768},{768,896... | collective-permute-start | bytes 688136 | tf_op jit(solution)/shard_map/ppermute | solution.py:45
  103.3 9.1 %collective-permute-start.6 = (bf16[128,896]{1,0:T(8,128)(2,1)S(1)}, bf16[128,896]{1,0:T(8,128)(2,1)S(1)}, u32[]{:S(2)}, u32[]{:S(2)}) collective-permute-start(bf16[128,896]{1,0:T(8,128)(2,1)S(1)} %collective-permute-done.4), channel_id=1, source_target_pairs={{0,128},{128,256},{256,384},{384,512},{512,640},{640,768},{768,896... | collective-permute-start | bytes 688136 | tf_op jit(solution)/shard_map/ppermute | solution.py:45
  113.7 29.9 %all-to-all-start.2 = ((bf16[8,128,128]{2,1,0:T(8,128)(2,1)}), bf16[8,128,128]{2,1,0:T(8,128)(2,1)S(1)}, u32[]{:S(2)}, u32[]{:S(2)}) async-start(bf16[8,128,128]{2,1,0:T(8,128)(2,1)} %broadcast_in_dim.60), calls=%async_computation.2 | async-start | bytes 524288 | tf_op jit(solution)/shard_map/all_to_all | solution.py:15
  121.1 23.6 %collective-permute-start.7 = (bf16[128,896]{1,0:T(8,128)(2,1)}, bf16[128,896]{1,0:T(8,128)(2,1)}, u32[]{:S(2)}, u32[]{:S(2)}) collective-permute-start(bf16[128,896]{1,0:T(8,128)(2,1)} %get-tuple-element.11), channel_id=1, source_target_pairs={{0,128},{128,256},{256,384},{384,512},{512,640},{640,768},{768,896... | collective-permute-start | bytes 688136 | tf_op jit(solution)/shard_map/ppermute | solution.py:69
  124.9 23.5 %collective-permute-start.9 = (bf16[128,896]{1,0:T(8,128)(2,1)S(1)}, bf16[128,896]{1,0:T(8,128)(2,1)}, u32[]{:S(2)}, u32[]{:S(2)}) collective-permute-start(bf16[128,896]{1,0:T(8,128)(2,1)S(1)} %get-tuple-element.10), channel_id=1, source_target_pairs={{0,384},{128,512},{256,640},{384,768},{512,896},{640,0},{768,128},... | collective-permute-start | bytes 688136 | tf_op jit(solution)/shard_map/ppermute | solution.py:69
  131.3 30.4 %collective-permute-start.10 = (bf16[128,896]{1,0:T(8,128)(2,1)S(1)}, bf16[128,896]{1,0:T(8,128)(2,1)}, u32[]{:S(2)}, u32[]{:S(2)}) collective-permute-start(bf16[128,896]{1,0:T(8,128)(2,1)S(1)} %get-tuple-element.9), channel_id=1, source_target_pairs={{0,512},{128,640},{256,768},{384,896},{512,0},{640,128},{768,256},... | collective-permute-start | bytes 688136 | tf_op jit(solution)/shard_map/ppermute | solution.py:69
  133.3 31.1 %collective-permute-start.11 = (bf16[128,896]{1,0:T(8,128)(2,1)S(1)}, bf16[128,896]{1,0:T(8,128)(2,1)}, u32[]{:S(2)}, u32[]{:S(2)}) collective-permute-start(bf16[128,896]{1,0:T(8,128)(2,1)S(1)} %get-tuple-element.8), channel_id=1, source_target_pairs={{0,640},{128,768},{256,896},{384,0},{512,128},{640,256},{768,384},... | collective-permute-start | bytes 688136 | tf_op jit(solution)/shard_map/ppermute | solution.py:69
  140.2 25.4 %collective-permute-start.12 = (bf16[128,896]{1,0:T(8,128)(2,1)S(1)}, bf16[128,896]{1,0:T(8,128)(2,1)}, u32[]{:S(2)}, u32[]{:S(2)}) collective-permute-start(bf16[128,896]{1,0:T(8,128)(2,1)S(1)} %get-tuple-element.7), channel_id=1, source_target_pairs={{0,768},{128,896},{256,0},{384,128},{512,256},{640,384},{768,512},... | collective-permute-start | bytes 688136 | tf_op jit(solution)/shard_map/ppermute | solution.py:69
  144.7 24.4 %collective-permute-start.13 = (bf16[128,896]{1,0:T(8,128)(2,1)S(1)}, bf16[128,896]{1,0:T(8,128)(2,1)S(1)}, u32[]{:S(2)}, u32[]{:S(2)}) collective-permute-start(bf16[128,896]{1,0:T(8,128)(2,1)S(1)} %get-tuple-element.6), channel_id=1, source_target_pairs={{0,896},{128,0},{256,128},{384,256},{512,384},{640,512},{768,640},... | collective-permute-start | bytes 688136 | tf_op jit(solution)/shard_map/ppermute | solution.py:69
  148.4 21.0 %collective-permute-start.8 = (bf16[128,896]{1,0:T(8,128)(2,1)S(1)}, bf16[128,896]{1,0:T(8,128)(2,1)S(1)}, u32[]{:S(2)}, u32[]{:S(2)}) collective-permute-start(bf16[128,896]{1,0:T(8,128)(2,1)S(1)} %get-tuple-element.5), channel_id=1, source_target_pairs={{0,256},{128,384},{256,512},{384,640},{512,768},{640,896},{768,0},... | collective-permute-start | bytes 688136 | tf_op jit(solution)/shard_map/ppermute | solution.py:69
  169.3 7.9 %copy-start.2 = (s32[1,64,8]{1,2,0:T(8,128)S(1)}, s32[1,64,8]{1,2,0:T(8,128)}, u32[]{:S(2)}) copy-start(s32[1,64,8]{1,2,0:T(8,128)} %param.8) | copy-start | bytes 6148
  169.3 7.9 %copy-start.3 = (s32[1,64,8]{1,2,0:T(8,128)S(1)}, s32[1,64,8]{1,2,0:T(8,128)}, u32[]{:S(2)}) copy-start(s32[1,64,8]{1,2,0:T(8,128)} %param.7) | copy-start | bytes 6148
  170.4 28.2 %all-to-all-start.3 = ((bf16[32,4,896]{2,1,0:T(4,128)(2,1)}), bf16[32,4,896]{2,1,0:T(4,128)(2,1)S(1)}, u32[]{:S(2)}, u32[]{:S(2)}) async-start(bf16[32,4,896]{2,1,0:T(4,128)(2,1)} %reshape.52), calls=%async_computation.3 | async-start | bytes 458752 | tf_op jit(solution)/shard_map/all_to_all | solution.py:15
  216.6 0.6 copy-start.4

commit v2 on v1

--- a/solution.py
+++ b/solution.py
@@ -1,6 +1,8 @@
 import jax
 import jax.numpy as jnp
 from jax import lax
+from jax.experimental import pallas as pl
+from jax.experimental.pallas import tpu as pltpu
 from jax.sharding import Mesh
 from jax.sharding import PartitionSpec as P
 
@@ -15,9 +17,87 @@
     return lax.all_to_all(parts, axes, 0, 0, tiled=True)
 
 
-def in_columns(rows, pieces):
-    cols = rows.shape[1] // pieces
-    return jnp.stack([rows[:, i * cols : (i + 1) * cols] for i in range(pieces)])
+def vmem():
+    return pl.BlockSpec(memory_space=pltpu.VMEM)
+
+
+def in_vmem(x):
+    return pltpu.with_memory_space_constraint(x, pltpu.VMEM)
+
+
+def anywhere():
+    return pl.BlockSpec(memory_space=pl.ANY)
+
+
+def in_columns(rows, pieces, copies):
+    own, width = rows.shape
+    cols = width // pieces
+
+    def kernel(rows_ref, out_ref):
+        for i in range(pieces):
+            piece = rows_ref[:, i * cols : (i + 1) * cols]
+            for j in range(copies):
+                out_ref[i * copies + j] = piece
+
+    return pl.pallas_call(
+        kernel,
+        out_shape=jax.ShapeDtypeStruct((pieces * copies, own, cols), rows.dtype),
+        in_specs=[vmem()],
+        out_specs=vmem(),
+        name="in_columns",
+    )(rows)
+
+
+def cut_ahead(matrix, axis):
+    n = lax.axis_size(axis)
+    rows, width = matrix.shape
+    cols = width // n
+
+    def kernel(matrix_ref, *refs):
+        outs, sems = refs[:n], refs[n]
+        here = lax.axis_index(axis)
+        copies = []
+        for k in range(n):
+            at = pl.multiple_of(lax.rem(here + k, n) * cols, cols)
+            copies.append(
+                pltpu.make_async_copy(matrix_ref.at[:, pl.ds(at, cols)], outs[k], sems.at[k])
+            )
+        for copy in copies:
+            copy.start()
+        for copy in copies:
+            copy.wait()
+
+    return pl.pallas_call(
+        kernel,
+        out_shape=[jax.ShapeDtypeStruct((rows, cols), matrix.dtype)] * n,
+        in_specs=[anywhere()],
+        out_specs=[anywhere()] * n,
+        scratch_shapes=[pltpu.SemaphoreType.DMA((n,))],
+        name="cut_ahead",
+    )(matrix)
+
+
+def down_product(hiddens, downs, axis):
+    n = lax.axis_size(axis)
+    rows = hiddens.shape[1]
+    cols = downs[0].shape[1]
+
+    def kernel(hid_ref, *refs):
+        outs_ref = refs[n]
+        here = lax.axis_index(axis)
+        total = jnp.zeros((rows, cols), jnp.float32)
+        for k in range(n):
+            part = hid_ref[lax.rem(here - k + n, n)]
+            total += jnp.dot(part, refs[k][...], preferred_element_type=jnp.float32)
+        outs_ref[...] = total.astype(outs_ref.dtype)
+
+    return pl.pallas_call(
+        kernel,
+        out_shape=jax.ShapeDtypeStruct((rows, cols), jnp.bfloat16),
+        in_specs=[vmem()] * (n + 1),
+        out_specs=vmem(),
+        name="down_product",
+    )(*(in_vmem(x) for x in (hiddens, *downs)))
 
 
 def routing(expert_ids, gate_codes, experts, capacity):
@@ -58,16 +138,10 @@
     hid = w_gate.shape[2]
     here = lax.axis_index("y")
 
-    blocks = in_columns(tokens[0], ny)
-    blocks = jnp.broadcast_to(blocks[:, None], (ny, nh, own, cols))
-    toks = exchange(blocks.reshape(ny * nh, own, cols), GROUP)
-    blocks = [w_down[0][:, i * cols : (i + 1) * cols] for i in range(ny)]
-    blocks = jnp.stack(blocks)
-    downs = {}
-    for k in sorted(range(1, ny), key=lambda k: -min(k, ny - k)):
-        block = lax.dynamic_index_in_dim(blocks, lax.rem(here + k, ny), 0, keepdims=False)
-        downs[k] = lax.ppermute(block, "y", [(i, (i + k) % ny) for i in range(ny)])
-    downs[0] = lax.dynamic_index_in_dim(blocks, here, 0, keepdims=False)
+    toks = exchange(in_columns(tokens[0], ny, nh), GROUP)
+    downs = list(cut_ahead(w_down[0], "y"))
+    for k in range(1, ny):
+        downs[k] = lax.ppermute(downs[k], "y", [(i, (i + k) % ny) for i in range(ny)])
 
     place, weight = routing(expert_ids[0], gate_codes[0], experts, CAPG)
     mix = jnp.where(place, weight[..., None], jnp.float32(0.0))
@@ -91,11 +165,7 @@
         second += jnp.dot(shard, up, preferred_element_type=jnp.float32)
     hidden = (jax.nn.silu(first) * second).astype(jnp.bfloat16)
     hiddens = exchange(jnp.broadcast_to(hidden[None], (ny, count, hid)), "y")
-    outs = jnp.float32(0.0)
-    for k in range(ny):
-        part = lax.dynamic_index_in_dim(hiddens, lax.rem(here - k + ny, ny), 0, keepdims=False)
-        outs += jnp.dot(part, downs[k], preferred_element_type=jnp.float32)
-    outs = outs.astype(jnp.bfloat16)
+    outs = down_product(hiddens, downs, "y")
     back = exchange(outs.reshape(sets, CAPG, cols), EXPERT)
     mixed = jnp.einsum(
         "tej,ejc->tc",

time: 219 us -> 268 us (1.22)
  Pallas kernels: 0 us -> 59.6 us
  local copies, waits for them, and re-layouts: 25.2 us -> 4.07 us
  waiting for transfers between devices: 68.6 us -> 85 us
  matrix products: 13.6 us -> 6.16 us
  starting transfers between devices: 91.1 us -> 96.7 us
  blocking collectives: 17.4 us -> 14.5 us
    pallas_call x0 -> x3, Pallas kernels: none -> 59.6 us  [the longest x1 56.8 us: cut_ahead(): pl.pallas_call(kernel, out_shape=[jax.ShapeDtypeStruct((rows, cols), matr...]
    ppermute x3, waiting for transfers between devices: 3.16 us -> 20 us  [around(): b = lax.ppermute(b, axis, down)]
    unnamed x31 -> x27, local copies, waits for them, and re-layouts: 17.3 us -> 0.74 us
    all_to_all x4, waiting for transfers between devices: 41.2 us -> 31.4 us  [exchange(): return lax.all_to_all(parts, axes, 0, 0, tiled=True)]
    ppermute x7, waiting for transfers between devices: 11.8 us -> 21.6 us  [per_device(): lax.ppermute(downs[k], 'y', [(i, (i + k) % ny) for i in range(ny)])]
    all_to_all x4, starting transfers between devices: 38.2 us -> 45.7 us  [exchange(): return lax.all_to_all(parts, axes, 0, 0, tiled=True)]
    dot_general x8 -> x0, matrix products: 7.41 us -> none  [per_device(): outs += jnp.dot(part, downs[k], preferred_element_type=jnp.float32)]
    all_to_all x1, blocking collectives: 17.4 us -> 14.5 us  [exchange(): return lax.all_to_all(parts, axes, 0, 0, tiled=True)]
  transfers between devices with their start and end apart: 18 -> 18, of which waited for: 10 -> 11; matrix products, arithmetic and copies ran while one was open for 13% -> 3% of each run, Pallas kernels for 0% -> 21%
where the time goes in v2:
time: 268 us; the launch traced here: 267 us
  starting transfers between devices  96.7 us (36%)
  waiting for transfers between devices  85 us (32%)
  Pallas kernels  59.6 us (22%)
  blocking collectives  14.5 us (5%)
  matrix products  6.16 us (2%)
  local copies, waits for them, and re-layouts  4.07 us (2%)
    pallas_call x1, Pallas kernels, cut_ahead(): pl.pallas_call(kernel, out_shape=[jax.ShapeDtypeStruct((rows, cols), matr...  56.8 us
    all_to_all x4, starting transfers between devices, exchange(): return lax.all_to_all(parts, axes, 0, 0, tiled=True)  45.7 us
    all_to_all x4, waiting for transfers between devices, exchange(): return lax.all_to_all(parts, axes, 0, 0, tiled=True)  31.4 us
    ppermute x7, starting transfers between devices, per_device(): lax.ppermute(downs[k], 'y', [(i, (i + k) % ny) for i in range(ny)])  28.2 us
    ppermute x7, waiting for transfers between devices, per_device(): lax.ppermute(downs[k], 'y', [(i, (i + k) % ny) for i in range(ny)])  21.6 us
    ppermute x3, waiting for transfers between devices, around(): b = lax.ppermute(b, axis, down)  20 us
    all_to_all x1, blocking collectives, exchange(): return lax.all_to_all(parts, axes, 0, 0, tiled=True)  14.5 us
    ppermute x3, starting transfers between devices, around(): b = lax.ppermute(b, axis, down)  14.1 us
  transfers between devices with their start and end apart: 18, of which 11 were waited for; matrix products, arithmetic and copies ran while one was open for 3% of the time, Pallas kernels for 21%

profile of v2, /device:TPU:2, one launch (start us, length us, event | category | flops | bytes accessed | tf_op | source)
XLA Modules:
  0.0 267.3 jit_solution(3327938343570077096)
XLA Ops:
  0.0 1.5 in_columns.1
  1.5 8.8 %all-to-all-start = ((bf16[16,4,896]{2,1,0:T(4,128)(2,1)}), bf16[16,4,896]{2,1,0:T(4,128)(2,1)S(1)}, u32[]{:S(2)}, u32[]{:S(2)}) async-start(bf16[16,4,896]{2,1,0:T(4,128)(2,1)} %in_columns.1), calls=%async_computation | async-start | bytes 229376 | tf_op jit(solution)/shard_map/all_to_all | solution.py:17
  10.3 0.7 fusion.44
  11.2 10.1 %all-to-all-done = bf16[16,4,896]{2,1,0:T(4,128)(2,1)S(1)} async-done(((bf16[16,4,896]{2,1,0:T(4,128)(2,1)}), bf16[16,4,896]{2,1,0:T(4,128)(2,1)S(1)}, u32[]{:S(2)}, u32[]{:S(2)}) %all-to-all-start) | async-done | bytes 114720 | tf_op jit(solution)/shard_map/all_to_all | solution.py:17
  21.5 0.8 copy.18
  22.3 19.3 %all-to-all-start.1 = ((bf16[32,4,896]{2,1,0:T(4,128)(2,1)}), bf16[32,4,896]{2,1,0:T(4,128)(2,1)S(1)}, u32[]{:S(2)}, u32[]{:S(2)}) async-start(bf16[32,4,896]{2,1,0:T(4,128)(2,1)} %copy.18), calls=%async_computation.1 | async-start | bytes 458752 | tf_op jit(solution)/shard_map/all_to_all | solution.py:17
  41.6 56.8 %cut_ahead.1 = (bf16[128,896]{1,0:T(8,128)(2,1)}, bf16[128,896]{1,0:T(8,128)(2,1)}, bf16[128,896]{1,0:T(8,128)(2,1)}, bf16[128,896]{1,0:T(8,128)(2,1)}, bf16[128...) custom-call(bf16[128,7168]{1,0:T(8,128)(2,1)} %bitcast.114), custom_call_target="tpu_custom_call" | custom-call | tf_op jit(solution)/shard_map/cut_ahead/pallas_call | solution.py:70
  98.3 2.7 %collective-permute-start.10 = (bf16[128,896]{1,0:T(8,128)(2,1)}, bf16[128,896]{1,0:T(8,128)(2,1)S(1)}, u32[]{:S(2)}, u32[]{:S(2)}) collective-permute-start(bf16[128,896]{1,0:T(8,128)(2,1)} %get-tuple-element.17), channel_id=1, source_target_pairs={{0,512},{128,640},{256,768},{384,896},{512,0},{640,128},{768,256},... | collective-permute-start | bytes 688136 | tf_op jit(solution)/shard_map/ppermute | solution.py:144
  101.0 6.0 %collective-permute-start.11 = (bf16[128,896]{1,0:T(8,128)(2,1)}, bf16[128,896]{1,0:T(8,128)(2,1)S(1)}, u32[]{:S(2)}, u32[]{:S(2)}) collective-permute-start(bf16[128,896]{1,0:T(8,128)(2,1)} %get-tuple-element.18), channel_id=1, source_target_pairs={{0,640},{128,768},{256,896},{384,0},{512,128},{640,256},{768,384},... | collective-permute-start | bytes 688136 | tf_op jit(solution)/shard_map/ppermute | solution.py:144
  107.2 2.8 %collective-permute-start = (bf16[128,896]{1,0:T(8,128)(2,1)S(1)}, bf16[128,896]{1,0:T(8,128)(2,1)S(1)}, u32[]{:S(2)}, u32[]{:S(2)}) collective-permute-start(bf16[128,896]{1,0:T(8,128)(2,1)S(1)} %reshape.46), channel_id=1, source_target_pairs={{0,128},{128,256},{256,384},{384,512},{512,640},{640,768},{768,896... | collective-permute-start | bytes 688136 | tf_op jit(solution)/shard_map/ppermute | solution.py:125
  110.0 4.4 %collective-permute-start.1 = (bf16[128,896]{1,0:T(8,128)(2,1)S(1)}, bf16[128,896]{1,0:T(8,128)(2,1)S(1)}, u32[]{:S(2)}, u32[]{:S(2)}) collective-permute-start(bf16[128,896]{1,0:T(8,128)(2,1)S(1)} %reshape.46), channel_id=1, source_target_pairs={{0,896},{128,0},{256,128},{384,256},{512,384},{640,512},{768,640},... | collective-permute-start | bytes 688136 | tf_op jit(solution)/shard_map/ppermute | solution.py:128
  114.4 1.2 fusion.14
  115.8 17.1 %collective-permute-done.1 = bf16[128,896]{1,0:T(8,128)(2,1)S(1)} collective-permute-done((bf16[128,896]{1,0:T(8,128)(2,1)S(1)}, bf16[128,896]{1,0:T(8,128)(2,1)S(1)}, u32[]{:S(2)}, u32[]{:S(2)}) %collective-permute-start.1) | collective-permute-done | bytes 229408 | tf_op jit(solution)/shard_map/ppermute | solution.py:128
  132.9 4.5 %collective-permute-start.3 = (bf16[128,896]{1,0:T(8,128)(2,1)S(1)}, bf16[128,896]{1,0:T(8,128)(2,1)S(1)}, u32[]{:S(2)}, u32[]{:S(2)}) collective-permute-start(bf16[128,896]{1,0:T(8,128)(2,1)S(1)} %collective-permute-done.1), channel_id=1, source_target_pairs={{0,896},{128,0},{256,128},{384,256},{512,384},{640,512},{768,640},... | collective-permute-start | bytes 688136 | tf_op jit(solution)/shard_map/ppermute | solution.py:128
  137.5 1.9 collective-permute-start.2
  139.4 1.2 convolution_add_fusion.4
  140.8 0.2 convolution_add_fusion.3
  141.0 0.2 convolution_add_fusion.8
  141.3 1.5 collective-permute-done.3
  142.8 5.3 %collective-permute-start.5 = (bf16[128,896]{1,0:T(8,128)(2,1)S(1)}, bf16[128,896]{1,0:T(8,128)(2,1)S(1)}, u32[]{:S(2)}, u32[]{:S(2)}) collective-permute-start(bf16[128,896]{1,0:T(8,128)(2,1)S(1)} %collective-permute-done.3), channel_id=1, source_target_pairs={{0,896},{128,0},{256,128},{384,256},{512,384},{640,512},{768,640},... | collective-permute-start | bytes 688136 | tf_op jit(solution)/shard_map/ppermute | solution.py:128
  148.5 1.9 collective-permute-start.4
  150.5 0.2 fusion.2
  150.7 0.2 fusion.4
  150.9 1.3 collective-permute-done.5
  152.8 5.3 %collective-permute-done.4 = bf16[128,896]{1,0:T(8,128)(2,1)S(1)} collective-permute-done((bf16[128,896]{1,0:T(8,128)(2,1)S(1)}, bf16[128,896]{1,0:T(8,128)(2,1)S(1)}, u32[]{:S(2)}, u32[]{:S(2)}) %collective-permute-start.4) | collective-permute-done | bytes 229408 | tf_op jit(solution)/shard_map/ppermute | solution.py:125
  158.0 1.9 collective-permute-start.6
  160.0 0.2 fusion.1
  160.2 0.2 fusion.3
  160.4 6.7 %collective-permute-done.6 = bf16[128,896]{1,0:T(8,128)(2,1)S(1)} collective-permute-done((bf16[128,896]{1,0:T(8,128)(2,1)S(1)}, bf16[128,896]{1,0:T(8,128)(2,1)S(1)}, u32[]{:S(2)}, u32[]{:S(2)}) %collective-permute-start.6) | collective-permute-done | bytes 229408 | tf_op jit(solution)/shard_map/ppermute | solution.py:125
  167.4 0.2 multiply_convert_fusion
  167.6 0.7 broadcast_in_dim.53
  168.4 5.7 %all-to-all-start.2 = ((bf16[8,128,128]{2,1,0:T(8,128)(2,1)}), bf16[8,128,128]{2,1,0:T(8,128)(2,1)S(1)}, u32[]{:S(2)}, u32[]{:S(2)}) async-start(bf16[8,128,128]{2,1,0:T(8,128)(2,1)} %broadcast_in_dim.53), calls=%async_computation.2 | async-start | bytes 524288 | tf_op jit(solution)/shard_map/all_to_all | solution.py:17
  174.0 6.0 %collective-permute-start.12 = (bf16[128,896]{1,0:T(8,128)(2,1)}, bf16[128,896]{1,0:T(8,128)(2,1)S(1)}, u32[]{:S(2)}, u32[]{:S(2)}) collective-permute-start(bf16[128,896]{1,0:T(8,128)(2,1)} %get-tuple-element.19), channel_id=1, source_target_pairs={{0,768},{128,896},{256,0},{384,128},{512,256},{640,384},{768,512},... | collective-permute-start | bytes 688136 | tf_op jit(solution)/shard_map/ppermute | solution.py:144
  180.1 3.4 %collective-permute-start.13 = (bf16[128,896]{1,0:T(8,128)(2,1)S(1)}, bf16[128,896]{1,0:T(8,128)(2,1)S(1)}, u32[]{:S(2)}, u32[]{:S(2)}) collective-permute-start(bf16[128,896]{1,0:T(8,128)(2,1)S(1)} %copy-done.9), channel_id=1, source_target_pairs={{0,896},{128,0},{256,128},{384,256},{512,384},{640,512},{768,640},... | collective-permute-start | bytes 688136 | tf_op jit(solution)/shard_map/ppermute | solution.py:144
  183.4 2.5 collective-permute-start.7
  185.9 1.9 collective-permute-start.8
  187.9 5.7 %collective-permute-start.9 = (bf16[128,896]{1,0:T(8,128)(2,1)S(1)}, bf16[128,896]{1,0:T(8,128)(2,1)S(1)}, u32[]{:S(2)}, u32[]{:S(2)}) collective-permute-start(bf16[128,896]{1,0:T(8,128)(2,1)S(1)} %copy-done.6), channel_id=1, source_target_pairs={{0,384},{128,512},{256,640},{384,768},{512,896},{640,0},{768,128},... | collective-permute-start | bytes 688136 | tf_op jit(solution)/shard_map/ppermute | solution.py:144
  193.6 0.7 collective-permute-done.13.refs_7_
  194.4 2.5 collective-permute-done.7.refs_1_
  196.8 9.3 %collective-permute-done.8.refs_2_ = bf16[128,896]{1,0:T(8,128)(2,1)S(1)} collective-permute-done((bf16[128,896]{1,0:T(8,128)(2,1)S(1)}, bf16[128,896]{1,0:T(8,128)(2,1)S(1)}, u32[]{:S(2)}, u32[]{:S(2)}) %collective-permute-start.8) | collective-permute-done | bytes 229408 | tf_op jit(solution)/shard_map/ppermute | solution.py:144
  206.2 9.1 %collective-permute-done.9.refs_3_ = bf16[128,896]{1,0:T(8,128)(2,1)S(1)} collective-permute-done((bf16[128,896]{1,0:T(8,128)(2,1)S(1)}, bf16[128,896]{1,0:T(8,128)(2,1)S(1)}, u32[]{:S(2)}, u32[]{:S(2)}) %collective-permute-start.9) | collective-permute-done | bytes 229408 | tf_op jit(solution)/shard_map/ppermute | solution.py:144
  215.3 1.3 down_product.1
  216.6 1.7 reshape.47
  218.2 12.0 %all-to-all-start.3 = ((bf16[32,4,896]{2,1,0:T(4,128)(2,1)}), bf16[32,4,896]{2,1,0:T(4,128)(2,1)S(1)}, u32[]{:S(2)}, u32[]{:S(2)}) async-start(bf16[32,4,896]{2,1,0:T(4,128)(2,1)} %reshape.47), calls=%async_computation.3 | async-start | bytes 458752 | tf_op jit(solution)/shard_map/all_to_all | solution.py:17
  230.3 21.3 %all-to-all-done.3 = bf16[32,4,896]{2,1,0:T(4,128)(2,1)S(1)} async-done(((bf16[32,4,896]{2,1,0:T(4,128)(2,1)}), bf16[32,4,896]{2,1,0:T(4,128)(2,1)S(1)}, u32[]{:S(2)}, u32[]{:S(2)}) %all-to-all-start.3) | async-done | bytes 229408 | tf_op jit(solution)/shard_map/all_to_all | solution.py:17
  251.7 0.3 fusion
  252.0 14.5 %all_to_all.25 = bf16[16,4,896]{2,1,0:T(4,128)(2,1)S(1)} all-to-all(bf16[16,4,896]{2,1,0:T(4,128)(2,1)S(1)} %reshape.48), channel_id=1, replica_groups=mesh['y'=8,'xh'=2,'z'=16,'core'=2,'dp'=2] {'y','xh'}, dimensions={0} | all-to-all | bytes 229376 | tf_op jit(solution)/shard_map/all_to_all | solution.py:17
  266.7 0.6 copy-done.5
  (51 shorter events, 2.3 us)
Async XLA Ops:
  1.5 19.8 %all-to-all-start = ((bf16[16,4,896]{2,1,0:T(4,128)(2,1)}), bf16[16,4,896]{2,1,0:T(4,128)(2,1)S(1)}, u32[]{:S(2)}, u32[]{:S(2)}) async-start(bf16[16,4,896]{2,1,0:T(4,128)(2,1)} %in_columns.1), calls=%async_computation | async-start | bytes 229376 | tf_op jit(solution)/shard_map/all_to_all | solution.py:17
  22.3 93.3 %copy-start.1 = (bf16[1,7168,128]{2,1,0:T(8,128)(2,1)S(1)}, bf16[1,7168,128]{2,1,0:T(8,128)(2,1)}, u32[]{:S(2)}) copy-start(bf16[1,7168,128]{2,1,0:T(8,128)(2,1)} %param.9) | copy-start | bytes 5505028
  22.3 84.9 %all-to-all-start.1 = ((bf16[32,4,896]{2,1,0:T(4,128)(2,1)}), bf16[32,4,896]{2,1,0:T(4,128)(2,1)S(1)}, u32[]{:S(2)}, u32[]{:S(2)}) async-start(bf16[32,4,896]{2,1,0:T(4,128)(2,1)} %copy.18), calls=%async_computation.1 | async-start | bytes 458752 | tf_op jit(solution)/shard_map/all_to_all | solution.py:17
  98.3 87.6 %collective-permute-start.10 = (bf16[128,896]{1,0:T(8,128)(2,1)}, bf16[128,896]{1,0:T(8,128)(2,1)S(1)}, u32[]{:S(2)}, u32[]{:S(2)}) collective-permute-start(bf16[128,896]{1,0:T(8,128)(2,1)} %get-tuple-element.17), channel_id=1, source_target_pairs={{0,512},{128,640},{256,768},{384,896},{512,0},{640,128},{768,256},... | collective-permute-start | bytes 688136 | tf_op jit(solution)/shard_map/ppermute | solution.py:144
  101.0 86.8 %collective-permute-start.11 = (bf16[128,896]{1,0:T(8,128)(2,1)}, bf16[128,896]{1,0:T(8,128)(2,1)S(1)}, u32[]{:S(2)}, u32[]{:S(2)}) collective-permute-start(bf16[128,896]{1,0:T(8,128)(2,1)} %get-tuple-element.18), channel_id=1, source_target_pairs={{0,640},{128,768},{256,896},{384,0},{512,128},{640,256},{768,384},... | collective-permute-start | bytes 688136 | tf_op jit(solution)/shard_map/ppermute | solution.py:144
  107.2 33.6 %copy-start.2 = (bf16[1,7168,128]{2,1,0:T(8,128)(2,1)S(1)}, bf16[1,7168,128]{2,1,0:T(8,128)(2,1)}, u32[]{:S(2)}) copy-start(bf16[1,7168,128]{2,1,0:T(8,128)(2,1)} %param.10) | copy-start | bytes 5505028
  107.2 30.3 %collective-permute-start = (bf16[128,896]{1,0:T(8,128)(2,1)S(1)}, bf16[128,896]{1,0:T(8,128)(2,1)S(1)}, u32[]{:S(2)}, u32[]{:S(2)}) collective-permute-start(bf16[128,896]{1,0:T(8,128)(2,1)S(1)} %reshape.46), channel_id=1, source_target_pairs={{0,128},{128,256},{256,384},{384,512},{512,640},{640,768},{768,896... | collective-permute-start | bytes 688136 | tf_op jit(solution)/shard_map/ppermute | solution.py:125
  110.0 22.9 %collective-permute-start.1 = (bf16[128,896]{1,0:T(8,128)(2,1)S(1)}, bf16[128,896]{1,0:T(8,128)(2,1)S(1)}, u32[]{:S(2)}, u32[]{:S(2)}) collective-permute-start(bf16[128,896]{1,0:T(8,128)(2,1)S(1)} %reshape.46), channel_id=1, source_target_pairs={{0,896},{128,0},{256,128},{384,256},{512,384},{640,512},{768,640},... | collective-permute-start | bytes 688136 | tf_op jit(solution)/shard_map/ppermute | solution.py:128
  132.9 9.9 %collective-permute-start.3 = (bf16[128,896]{1,0:T(8,128)(2,1)S(1)}, bf16[128,896]{1,0:T(8,128)(2,1)S(1)}, u32[]{:S(2)}, u32[]{:S(2)}) collective-permute-start(bf16[128,896]{1,0:T(8,128)(2,1)S(1)} %collective-permute-done.1), channel_id=1, source_target_pairs={{0,896},{128,0},{256,128},{384,256},{512,384},{640,512},{768,640},... | collective-permute-start | bytes 688136 | tf_op jit(solution)/shard_map/ppermute | solution.py:128
  137.5 11.1 %collective-permute-start.2 = (bf16[128,896]{1,0:T(8,128)(2,1)S(1)}, bf16[128,896]{1,0:T(8,128)(2,1)S(1)}, u32[]{:S(2)}, u32[]{:S(2)}) collective-permute-start(bf16[128,896]{1,0:T(8,128)(2,1)S(1)} %collective-permute-done), channel_id=1, source_target_pairs={{0,128},{128,256},{256,384},{384,512},{512,640},{640,768},{768,896... | collective-permute-start | bytes 688136 | tf_op jit(solution)/shard_map/ppermute | solution.py:125
  142.8 9.4 %collective-permute-start.5 = (bf16[128,896]{1,0:T(8,128)(2,1)S(1)}, bf16[128,896]{1,0:T(8,128)(2,1)S(1)}, u32[]{:S(2)}, u32[]{:S(2)}) collective-permute-start(bf16[128,896]{1,0:T(8,128)(2,1)S(1)} %collective-permute-done.3), channel_id=1, source_target_pairs={{0,896},{128,0},{256,128},{384,256},{512,384},{640,512},{768,640},... | collective-permute-start | bytes 688136 | tf_op jit(solution)/shard_map/ppermute | solution.py:128
  148.5 9.5 %collective-permute-start.4 = (bf16[128,896]{1,0:T(8,128)(2,1)S(1)}, bf16[128,896]{1,0:T(8,128)(2,1)S(1)}, u32[]{:S(2)}, u32[]{:S(2)}) collective-permute-start(bf16[128,896]{1,0:T(8,128)(2,1)S(1)} %collective-permute-done.2), channel_id=1, source_target_pairs={{0,128},{128,256},{256,384},{384,512},{512,640},{640,768},{768,896... | collective-permute-start | bytes 688136 | tf_op jit(solution)/shard_map/ppermute | solution.py:125
  152.7 27.3 %copy-start.9 = (bf16[128,896]{1,0:T(8,128)(2,1)S(1)}, bf16[128,896]{1,0:T(8,128)(2,1)}, u32[]{:S(2)}) copy-start(bf16[128,896]{1,0:T(8,128)(2,1)} %get-tuple-element.20) | copy-start | bytes 688132
  152.7 30.7 %copy-start.8 = (bf16[128,896]{1,0:T(8,128)(2,1)S(1)}, bf16[128,896]{1,0:T(8,128)(2,1)}, u32[]{:S(2)}) copy-start(bf16[128,896]{1,0:T(8,128)(2,1)} %get-tuple-element.14) | copy-start | bytes 688132
  152.7 33.2 %copy-start.7 = (bf16[128,896]{1,0:T(8,128)(2,1)S(1)}, bf16[128,896]{1,0:T(8,128)(2,1)}, u32[]{:S(2)}) copy-start(bf16[128,896]{1,0:T(8,128)(2,1)} %get-tuple-element.15) | copy-start | bytes 688132
  152.7 35.2 %copy-start.6 = (bf16[128,896]{1,0:T(8,128)(2,1)S(1)}, bf16[128,896]{1,0:T(8,128)(2,1)}, u32[]{:S(2)}) copy-start(bf16[128,896]{1,0:T(8,128)(2,1)} %get-tuple-element.16) | copy-start | bytes 688132
  152.7 62.5 %copy-start = (bf16[128,896]{1,0:T(8,128)(2,1)S(1)}, bf16[128,896]{1,0:T(8,128)(2,1)}, u32[]{:S(2)}) copy-start(bf16[128,896]{1,0:T(8,128)(2,1)} %get-tuple-element.13.refs_0_) | copy-start | bytes 688132
  158.0 9.1 %collective-permute-start.6 = (bf16[128,896]{1,0:T(8,128)(2,1)S(1)}, bf16[128,896]{1,0:T(8,128)(2,1)S(1)}, u32[]{:S(2)}, u32[]{:S(2)}) collective-permute-start(bf16[128,896]{1,0:T(8,128)(2,1)S(1)} %collective-permute-done.4), channel_id=1, source_target_pairs={{0,128},{128,256},{256,384},{384,512},{512,640},{640,768},{768,896... | collective-permute-start | bytes 688136 | tf_op jit(solution)/shard_map/ppermute | solution.py:125
  168.3 61.9 %copy-start.3 = (s32[1,64,8]{1,2,0:T(8,128)S(1)}, s32[1,64,8]{1,2,0:T(8,128)}, u32[]{:S(2)}) copy-start(s32[1,64,8]{1,2,0:T(8,128)} %param.8) | copy-start | bytes 6148
  168.3 61.9 %copy-start.4 = (s32[1,64,8]{1,2,0:T(8,128)S(1)}, s32[1,64,8]{1,2,0:T(8,128)}, u32[]{:S(2)}) copy-start(s32[1,64,8]{1,2,0:T(8,128)} %param.7) | copy-start | bytes 6148
  168.4 46.9 %all-to-all-start.2 = ((bf16[8,128,128]{2,1,0:T(8,128)(2,1)}), bf16[8,128,128]{2,1,0:T(8,128)(2,1)S(1)}, u32[]{:S(2)}, u32[]{:S(2)}) async-start(bf16[8,128,128]{2,1,0:T(8,128)(2,1)} %broadcast_in_dim.53), calls=%async_computation.2 | async-start | bytes 524288 | tf_op jit(solution)/shard_map/all_to_all | solution.py:17
  174.0 19.6 %collective-permute-start.12 = (bf16[128,896]{1,0:T(8,128)(2,1)}, bf16[128,896]{1,0:T(8,128)(2,1)S(1)}, u32[]{:S(2)}, u32[]{:S(2)}) collective-permute-start(bf16[128,896]{1,0:T(8,128)(2,1)} %get-tuple-element.19), channel_id=1, source_target_pairs={{0,768},{128,896},{256,0},{384,128},{512,256},{640,384},{768,512},... | collective-permute-start | bytes 688136 | tf_op jit(solution)/shard_map/ppermute | solution.py:144
  180.1 14.3 %collective-permute-start.13 = (bf16[128,896]{1,0:T(8,128)(2,1)S(1)}, bf16[128,896]{1,0:T(8,128)(2,1)S(1)}, u32[]{:S(2)}, u32[]{:S(2)}) collective-permute-start(bf16[128,896]{1,0:T(8,128)(2,1)S(1)} %copy-done.9), channel_id=1, source_target_pairs={{0,896},{128,0},{256,128},{384,256},{512,384},{640,512},{768,640},... | collective-permute-start | bytes 688136 | tf_op jit(solution)/shard_map/ppermute | solution.py:144
  183.4 13.4 %collective-permute-start.7 = (bf16[128,896]{1,0:T(8,128)(2,1)S(1)}, bf16[128,896]{1,0:T(8,128)(2,1)S(1)}, u32[]{:S(2)}, u32[]{:S(2)}) collective-permute-start(bf16[128,896]{1,0:T(8,128)(2,1)S(1)} %copy-done.8), channel_id=1, source_target_pairs={{0,128},{128,256},{256,384},{384,512},{512,640},{640,768},{768,896... | collective-permute-start | bytes 688136 | tf_op jit(solution)/shard_map/ppermute | solution.py:144
  185.9 20.2 %collective-permute-start.8 = (bf16[128,896]{1,0:T(8,128)(2,1)S(1)}, bf16[128,896]{1,0:T(8,128)(2,1)S(1)}, u32[]{:S(2)}, u32[]{:S(2)}) collective-permute-start(bf16[128,896]{1,0:T(8,128)(2,1)S(1)} %copy-done.7), channel_id=1, source_target_pairs={{0,256},{128,384},{256,512},{384,640},{512,768},{640,896},{768,0},... | collective-permute-start | bytes 688136 | tf_op jit(solution)/shard_map/ppermute | solution.py:144
  187.9 27.4 %collective-permute-start.9 = (bf16[128,896]{1,0:T(8,128)(2,1)S(1)}, bf16[128,896]{1,0:T(8,128)(2,1)S(1)}, u32[]{:S(2)}, u32[]{:S(2)}) collective-permute-start(bf16[128,896]{1,0:T(8,128)(2,1)S(1)} %copy-done.6), channel_id=1, source_target_pairs={{0,384},{128,512},{256,640},{384,768},{512,896},{640,0},{768,128},... | collective-permute-start | bytes 688136 | tf_op jit(solution)/shard_map/ppermute | solution.py:144
  218.2 33.4 %all-to-all-start.3 = ((bf16[32,4,896]{2,1,0:T(4,128)(2,1)}), bf16[32,4,896]{2,1,0:T(4,128)(2,1)S(1)}, u32[]{:S(2)}, u32[]{:S(2)}) async-start(bf16[32,4,896]{2,1,0:T(4,128)(2,1)} %reshape.47), calls=%async_computation.3 | async-start | bytes 458752 | tf_op jit(solution)/shard_map/all_to_all | solution.py:17
  266.7 0.6 copy-start.5

commit v3 on v2

--- a/solution.py
+++ b/solution.py
@@ -17,6 +17,9 @@
     return lax.all_to_all(parts, axes, 0, 0, tiled=True)
 
 
+SMALL = pltpu.CompilerParams(vmem_limit_bytes=8 * 2**20)
+
+
 def vmem():
     return pl.BlockSpec(memory_space=pltpu.VMEM)
 
@@ -45,6 +48,7 @@
         in_specs=[vmem()],
         out_specs=vmem(),
         name="in_columns",
+        compiler_params=SMALL,
     )(rows)
 
 
@@ -69,12 +73,38 @@
 
     return pl.pallas_call(
         kernel,
-        out_shape=[jax.ShapeDtypeStruct((rows, cols), matrix.dtype)] * n,
+        out_shape=[pltpu.VMEM((rows, cols), matrix.dtype)] * n,
         in_specs=[anywhere()],
-        out_specs=[anywhere()] * n,
+        out_specs=[vmem()] * n,
         scratch_shapes=[pltpu.SemaphoreType.DMA((n,))],
         name="cut_ahead",
-    )(matrix)
+        compiler_params=SMALL,
+    )(pltpu.with_memory_space_constraint(matrix, pltpu.HBM))
+
+
+def gate_up_step(sums, shard, gate, up, step, axis):
+    n = lax.axis_size(axis)
+    rows, cols = shard.shape
+    hid = gate.shape[1]
+    first = sums is None
+
+    def kernel(*refs):
+        shard_ref, gate_ref, up_ref = refs[:3]
+        here = lax.axis_index(axis)
+        at = pl.multiple_of(lax.rem(here + step + n, n) * cols, cols)
+        block = shard_ref[...]
+        for i, weight in enumerate((gate_ref, up_ref)):
+            got = jnp.dot(block, weight[pl.ds(at, cols), :], preferred_element_type=jnp.float32)
+            refs[-2 + i][...] = got if first else refs[3 + i][...] + got
+
+    return pl.pallas_call(
+        kernel,
+        out_shape=[pltpu.VMEM((rows, hid), jnp.float32)] * 2,
+        in_specs=[vmem()] * (3 if first else 5),
+        out_specs=[vmem()] * 2,
+        name="gate_up_step",
+        compiler_params=SMALL,
+    )(*(in_vmem(x) for x in (shard, gate, up, *(sums or ()))))
 
 
 def down_product(hiddens, downs, axis):
@@ -97,6 +127,7 @@
         in_specs=[vmem()] * (n + 1),
         out_specs=vmem(),
         name="down_product",
+        compiler_params=SMALL,
     )(*(in_vmem(x) for x in (hiddens, *downs)))
 
 
@@ -136,7 +167,6 @@
     own, width = tokens.shape[1], tokens.shape[2]
     cols = width // ny
     hid = w_gate.shape[2]
-    here = lax.axis_index("y")
 
     toks = exchange(in_columns(tokens[0], ny, nh), GROUP)
     downs = list(cut_ahead(w_down[0], "y"))
@@ -154,15 +184,10 @@
     got = exchange(rows, EXPERT)
     sets = got.shape[0]
     count = sets * CAPG
-    gate_blocks = w_gate[0].reshape(ny, cols, hid)
-    up_blocks = w_up[0].reshape(ny, cols, hid)
-    first = second = jnp.float32(0.0)
+    sums = None
     for step, shard in around(got.reshape(count, cols), "y"):
-        at = lax.rem(here + step + ny, ny)
-        gate = lax.dynamic_index_in_dim(gate_blocks, at, 0, keepdims=False)
-        up = lax.dynamic_index_in_dim(up_blocks, at, 0, keepdims=False)
-        first += jnp.dot(shard, gate, preferred_element_type=jnp.float32)
-        second += jnp.dot(shard, up, preferred_element_type=jnp.float32)
+        sums = gate_up_step(sums, shard, w_gate[0], w_up[0], step, "y")
+    first, second = sums
     hidden = (jax.nn.silu(first) * second).astype(jnp.bfloat16)
     hiddens = exchange(jnp.broadcast_to(hidden[None], (ny, count, hid)), "y")
     outs = down_product(hiddens, downs, "y")

time: 268 us -> 201 us (0.75)
  Pallas kernels: 59.6 us -> 5.96 us
  blocking collectives: 14.5 us -> 54.9 us
  waiting for transfers between devices: 85 us -> 57.8 us
  starting transfers between devices: 96.7 us -> 73.3 us
  matrix products: 6.16 us -> 0.7 us
    pallas_call x1 -> x9, Pallas kernels: 56.8 us -> 4.69 us  [the longest x1 2.42 us: cut_ahead(): pl.pallas_call(kernel, out_shape=[pltpu.VMEM((rows, cols), matrix.dtype)]...]
    all_to_all x1 -> x2, blocking collectives: 14.5 us -> 54.9 us  [exchange(): return lax.all_to_all(parts, axes, 0, 0, tiled=True)]
    all_to_all x4 -> x3, starting transfers between devices: 45.7 us -> 23.7 us  [exchange(): return lax.all_to_all(parts, axes, 0, 0, tiled=True)]
    ppermute x3, waiting for transfers between devices: 20 us -> 0.01 us  [around(): b = lax.ppermute(b, axis, down)]
    dot_general x16 -> x0, matrix products: 5.46 us -> none  [the longest x8 3.67 us: per_device(): second += jnp.dot(shard, up, preferred_element_type=jnp.float32)]
    ppermute x4, waiting for transfers between devices: 12 us -> 7.58 us  [around(): a = lax.ppermute(a, axis, up)]
    unnamed x27 -> x25, local copies, waits for them, and re-layouts: 0.74 us -> 4.41 us
    ppermute x7, waiting for transfers between devices: 21.6 us -> 18.9 us  [per_device(): lax.ppermute(downs[k], 'y', [(i, (i + k) % ny) for i in range(ny)])]
  transfers between devices with their start and end apart: 18 -> 17, of which waited for: 11 -> 10; matrix products, arithmetic and copies ran while one was open for 3% -> 1% of each run, Pallas kernels for 21% -> 2%
where the time goes in v3:
time: 201 us; the launch traced here: 200 us
  starting transfers between devices  73.3 us (36%)
  waiting for transfers between devices  57.8 us (29%)
  blocking collectives  54.9 us (27%)
  local copies, waits for them, and re-layouts  6.16 us (3%)
  Pallas kernels  5.96 us (3%)
    all_to_all x2, blocking collectives, exchange(): return lax.all_to_all(parts, axes, 0, 0, tiled=True)  54.9 us
    all_to_all x3, waiting for transfers between devices, exchange(): return lax.all_to_all(parts, axes, 0, 0, tiled=True)  31.4 us
    ppermute x7, starting transfers between devices, per_device(): lax.ppermute(downs[k], 'y', [(i, (i + k) % ny) for i in range(ny)])  26.6 us
    all_to_all x3, starting transfers between devices, exchange(): return lax.all_to_all(parts, axes, 0, 0, tiled=True)  23.7 us
    ppermute x7, waiting for transfers between devices, per_device(): lax.ppermute(downs[k], 'y', [(i, (i + k) % ny) for i in range(ny)])  18.9 us
    ppermute x3, starting transfers between devices, around(): b = lax.ppermute(b, axis, down)  15 us
    ppermute x4, starting transfers between devices, around(): a = lax.ppermute(a, axis, up)  8.06 us
    ppermute x4, waiting for transfers between devices, around(): a = lax.ppermute(a, axis, up)  7.58 us
  transfers between devices with their start and end apart: 17, of which 10 were waited for; matrix products, arithmetic and copies ran while one was open for 1% of the time, Pallas kernels for 2%

profile of v3, /device:TPU:2, one launch (start us, length us, event | category | flops | bytes accessed | tf_op | source)
XLA Modules:
  0.0 200.2 jit_solution(9137662662681417689)
XLA Ops:
  0.0 0.8 copy-done.2
  0.8 0.6 in_columns.1
  1.5 8.8 %all-to-all-start = ((bf16[16,4,896]{2,1,0:T(4,128)(2,1)}), bf16[16,4,896]{2,1,0:T(4,128)(2,1)S(1)}, u32[]{:S(2)}, u32[]{:S(2)}) async-start(bf16[16,4,896]{2,1,0:T(4,128)(2,1)} %in_columns.1), calls=%async_computation | async-start | bytes 229376 | tf_op jit(solution)/shard_map/all_to_all | solution.py:17
  10.2 0.7 fusion.2
  11.2 10.1 %all-to-all-done = bf16[16,4,896]{2,1,0:T(4,128)(2,1)S(1)} async-done(((bf16[16,4,896]{2,1,0:T(4,128)(2,1)}), bf16[16,4,896]{2,1,0:T(4,128)(2,1)S(1)}, u32[]{:S(2)}, u32[]{:S(2)}) %all-to-all-start) | async-done | bytes 114720 | tf_op jit(solution)/shard_map/all_to_all | solution.py:17
  21.6 40.5 %all_to_all.25 = bf16[32,4,896]{2,1,0:T(4,128)(2,1)S(1)} all-to-all(bf16[32,4,896]{2,1,0:T(4,128)(2,1)S(1)} %copy.15), channel_id=1, replica_groups=mesh['y'=8,'xh'=2,'z'=16,'core'=2,'dp'=2] {'z','core'}, dimensions={0} | all-to-all | bytes 458752 | tf_op jit(solution)/shard_map/all_to_all | solution.py:17
  62.1 2.3 %collective-permute-start = (bf16[128,896]{1,0:T(8,128)(2,1)S(1)}, bf16[128,896]{1,0:T(8,128)(2,1)S(1)}, u32[]{:S(2)}, u32[]{:S(2)}) collective-permute-start(bf16[128,896]{1,0:T(8,128)(2,1)S(1)} %reshape.46.refs_0_), channel_id=1, source_target_pairs={{0,128},{128,256},{256,384},{384,512},{512,640},{640,768},{768,896... | collective-permute-start | bytes 688136 | tf_op jit(solution)/shard_map/ppermute | solution.py:156
  64.5 4.7 %collective-permute-start.4 = (bf16[128,896]{1,0:T(8,128)(2,1)S(1)}, bf16[128,896]{1,0:T(8,128)(2,1)S(1)}, u32[]{:S(2)}, u32[]{:S(2)}) collective-permute-start(bf16[128,896]{1,0:T(8,128)(2,1)S(1)} %reshape.46.refs_0_), channel_id=1, source_target_pairs={{0,896},{128,0},{256,128},{384,256},{512,384},{640,512},{768,640},... | collective-permute-start | bytes 688136 | tf_op jit(solution)/shard_map/ppermute | solution.py:159
  69.2 2.7 %collective-permute-done.refs_0_ = bf16[128,896]{1,0:T(8,128)(2,1)S(1)} collective-permute-done((bf16[128,896]{1,0:T(8,128)(2,1)S(1)}, bf16[128,896]{1,0:T(8,128)(2,1)S(1)}, u32[]{:S(2)}, u32[]{:S(2)}) %collective-permute-start) | collective-permute-done | bytes 229408 | tf_op jit(solution)/shard_map/ppermute | solution.py:156
  71.9 1.9 collective-permute-start.1
  73.9 5.1 %collective-permute-start.5 = (bf16[128,896]{1,0:T(8,128)(2,1)S(1)}, bf16[128,896]{1,0:T(8,128)(2,1)S(1)}, u32[]{:S(2)}, u32[]{:S(2)}) collective-permute-start(bf16[128,896]{1,0:T(8,128)(2,1)S(1)} %collective-permute-done.4.refs_0_), channel_id=1, source_target_pairs={{0,896},{128,0},{256,128},{384,256},{512,384},{640,512},{768,640},... | collective-permute-start | bytes 688136 | tf_op jit(solution)/shard_map/ppermute | solution.py:159
  79.0 2.0 %collective-permute-done.1.refs_0_ = bf16[128,896]{1,0:T(8,128)(2,1)S(1)} collective-permute-done((bf16[128,896]{1,0:T(8,128)(2,1)S(1)}, bf16[128,896]{1,0:T(8,128)(2,1)S(1)}, u32[]{:S(2)}, u32[]{:S(2)}) %collective-permute-start.1) | collective-permute-done | bytes 229408 | tf_op jit(solution)/shard_map/ppermute | solution.py:156
  81.0 1.9 collective-permute-start.2
  83.0 5.1 %collective-permute-start.6 = (bf16[128,896]{1,0:T(8,128)(2,1)S(1)}, bf16[128,896]{1,0:T(8,128)(2,1)S(1)}, u32[]{:S(2)}, u32[]{:S(2)}) collective-permute-start(bf16[128,896]{1,0:T(8,128)(2,1)S(1)} %collective-permute-done.5.refs_0_), channel_id=1, source_target_pairs={{0,896},{128,0},{256,128},{384,256},{512,384},{640,512},{768,640},... | collective-permute-start | bytes 688136 | tf_op jit(solution)/shard_map/ppermute | solution.py:159
  88.1 2.0 %collective-permute-done.2.refs_0_ = bf16[128,896]{1,0:T(8,128)(2,1)S(1)} collective-permute-done((bf16[128,896]{1,0:T(8,128)(2,1)S(1)}, bf16[128,896]{1,0:T(8,128)(2,1)S(1)}, u32[]{:S(2)}, u32[]{:S(2)}) %collective-permute-start.2) | collective-permute-done | bytes 229408 | tf_op jit(solution)/shard_map/ppermute | solution.py:156
  90.2 1.9 collective-permute-start.3
  92.1 2.4 %cut_ahead.1 = (bf16[128,896]{1,0:T(8,128)(2,1)S(1)}, bf16[128,896]{1,0:T(8,128)(2,1)S(1)}, bf16[128,896]{1,0:T(8,128)(2,1)S(1)}, bf16[128,896]{1,0:T(8,128)(2,1...) custom-call(bf16[128,7168]{1,0:T(8,128)(2,1)} %bitcast.65), custom_call_target="tpu_custom_call" | custom-call | tf_op jit(solution)/shard_map/cut_ahead/pallas_call | solution.py:74
  94.5 0.7 copy-done.3
  95.2 0.7 copy-done.5
  95.9 2.7 %collective-permute-start.10 = (bf16[128,896]{1,0:T(8,128)(2,1)}, bf16[128,896]{1,0:T(8,128)(2,1)S(1)}, u32[]{:S(2)}, u32[]{:S(2)}) collective-permute-start(bf16[128,896]{1,0:T(8,128)(2,1)} %get-tuple-element.49), channel_id=1, source_target_pairs={{0,512},{128,640},{256,768},{384,896},{512,0},{640,128},{768,256},... | collective-permute-start | bytes 688136 | tf_op jit(solution)/shard_map/ppermute | solution.py:174
  98.6 4.4 %collective-permute-start.11 = (bf16[128,896]{1,0:T(8,128)(2,1)}, bf16[128,896]{1,0:T(8,128)(2,1)S(1)}, u32[]{:S(2)}, u32[]{:S(2)}) collective-permute-start(bf16[128,896]{1,0:T(8,128)(2,1)} %get-tuple-element.50), channel_id=1, source_target_pairs={{0,640},{128,768},{256,896},{384,0},{512,128},{640,256},{768,384},... | collective-permute-start | bytes 688136 | tf_op jit(solution)/shard_map/ppermute | solution.py:174
  103.0 1.5 copy-done.1
  104.8 0.3 gate_up_step.9
  105.1 0.3 gate_up_step.10
  105.4 0.3 gate_up_step.11
  105.7 0.3 gate_up_step.12
  106.0 0.3 gate_up_step.13
  106.3 0.3 gate_up_step.14
  106.6 0.8 collective-permute-done.3.refs_0_
  107.3 0.3 gate_up_step.15
  107.6 0.7 broadcast_in_dim.53
  108.4 6.6 %all-to-all-start.2 = ((bf16[8,128,128]{2,1,0:T(8,128)(2,1)}), bf16[8,128,128]{2,1,0:T(8,128)(2,1)S(1)}, u32[]{:S(2)}, u32[]{:S(2)}) async-start(bf16[8,128,128]{2,1,0:T(8,128)(2,1)} %broadcast_in_dim.53), calls=%async_computation.2 | async-start | bytes 524288 | tf_op jit(solution)/shard_map/all_to_all | solution.py:17
  114.9 6.0 %collective-permute-start.12 = (bf16[128,896]{1,0:T(8,128)(2,1)}, bf16[128,896]{1,0:T(8,128)(2,1)S(1)}, u32[]{:S(2)}, u32[]{:S(2)}) collective-permute-start(bf16[128,896]{1,0:T(8,128)(2,1)} %copy-done.5), channel_id=1, source_target_pairs={{0,768},{128,896},{256,0},{384,128},{512,256},{640,384},{768,512},... | collective-permute-start | bytes 688136 | tf_op jit(solution)/shard_map/ppermute | solution.py:174
  121.0 3.4 %collective-permute-start.13 = (bf16[128,896]{1,0:T(8,128)(2,1)S(1)}, bf16[128,896]{1,0:T(8,128)(2,1)S(1)}, u32[]{:S(2)}, u32[]{:S(2)}) collective-permute-start(bf16[128,896]{1,0:T(8,128)(2,1)S(1)} %copy-done.4), channel_id=1, source_target_pairs={{0,896},{128,0},{256,128},{384,256},{512,384},{640,512},{768,640},... | collective-permute-start | bytes 688136 | tf_op jit(solution)/shard_map/ppermute | solution.py:174
  124.4 2.5 %collective-permute-start.7 = (bf16[128,896]{1,0:T(8,128)(2,1)S(1)}, bf16[128,896]{1,0:T(8,128)(2,1)S(1)}, u32[]{:S(2)}, u32[]{:S(2)}) collective-permute-start(bf16[128,896]{1,0:T(8,128)(2,1)S(1)} %get-tuple-element.46), channel_id=1, source_target_pairs={{0,128},{128,256},{256,384},{384,512},{512,640},{640,768},{768,896... | collective-permute-start | bytes 688136 | tf_op jit(solution)/shard_map/ppermute | solution.py:174
  126.9 1.9 collective-permute-start.8
  128.8 5.7 %collective-permute-start.9 = (bf16[128,896]{1,0:T(8,128)(2,1)S(1)}, bf16[128,896]{1,0:T(8,128)(2,1)S(1)}, u32[]{:S(2)}, u32[]{:S(2)}) collective-permute-start(bf16[128,896]{1,0:T(8,128)(2,1)S(1)} %get-tuple-element.48), channel_id=1, source_target_pairs={{0,384},{128,512},{256,640},{384,768},{512,896},{640,0},{768,128},... | collective-permute-start | bytes 688136 | tf_op jit(solution)/shard_map/ppermute | solution.py:174
  134.5 4.3 %collective-permute-done.12.refs_6_ = bf16[128,896]{1,0:T(8,128)(2,1)S(1)} collective-permute-done((bf16[128,896]{1,0:T(8,128)(2,1)}, bf16[128,896]{1,0:T(8,128)(2,1)S(1)}, u32[]{:S(2)}, u32[]{:S(2)}) %collective-permute-start.12) | collective-permute-done | bytes 229408 | tf_op jit(solution)/shard_map/ppermute | solution.py:174
  138.8 3.2 %collective-permute-done.13.refs_7_ = bf16[128,896]{1,0:T(8,128)(2,1)S(1)} collective-permute-done((bf16[128,896]{1,0:T(8,128)(2,1)S(1)}, bf16[128,896]{1,0:T(8,128)(2,1)S(1)}, u32[]{:S(2)}, u32[]{:S(2)}) %collective-permute-start.13) | collective-permute-done | bytes 229408 | tf_op jit(solution)/shard_map/ppermute | solution.py:174
  142.0 4.5 %collective-permute-done.8.refs_2_ = bf16[128,896]{1,0:T(8,128)(2,1)S(1)} collective-permute-done((bf16[128,896]{1,0:T(8,128)(2,1)S(1)}, bf16[128,896]{1,0:T(8,128)(2,1)S(1)}, u32[]{:S(2)}, u32[]{:S(2)}) %collective-permute-start.8) | collective-permute-done | bytes 229408 | tf_op jit(solution)/shard_map/ppermute | solution.py:174
  146.5 6.9 %collective-permute-done.9.refs_3_ = bf16[128,896]{1,0:T(8,128)(2,1)S(1)} collective-permute-done((bf16[128,896]{1,0:T(8,128)(2,1)S(1)}, bf16[128,896]{1,0:T(8,128)(2,1)S(1)}, u32[]{:S(2)}, u32[]{:S(2)}) %collective-permute-start.9) | collective-permute-done | bytes 229408 | tf_op jit(solution)/shard_map/ppermute | solution.py:174
  153.4 0.6 down_product.1
  154.0 0.8 reshape.47
  154.8 8.3 %all-to-all-start.3 = ((bf16[32,4,896]{2,1,0:T(4,128)(2,1)}), bf16[32,4,896]{2,1,0:T(4,128)(2,1)S(1)}, u32[]{:S(2)}, u32[]{:S(2)}) async-start(bf16[32,4,896]{2,1,0:T(4,128)(2,1)} %reshape.47), calls=%async_computation.3 | async-start | bytes 458752 | tf_op jit(solution)/shard_map/all_to_all | solution.py:17
  163.2 21.3 %all-to-all-done.3 = bf16[32,4,896]{2,1,0:T(4,128)(2,1)S(1)} async-done(((bf16[32,4,896]{2,1,0:T(4,128)(2,1)}), bf16[32,4,896]{2,1,0:T(4,128)(2,1)S(1)}, u32[]{:S(2)}, u32[]{:S(2)}) %all-to-all-start.3) | async-done | bytes 229408 | tf_op jit(solution)/shard_map/all_to_all | solution.py:17
  184.5 0.3 fusion
  184.9 14.5 %all_to_all.26 = bf16[16,4,896]{2,1,0:T(4,128)(2,1)S(1)} all-to-all(bf16[16,4,896]{2,1,0:T(4,128)(2,1)S(1)} %reshape.48), channel_id=1, replica_groups=mesh['y'=8,'xh'=2,'z'=16,'core'=2,'dp'=2] {'y','xh'}, dimensions={0} | all-to-all | bytes 229376 | tf_op jit(solution)/shard_map/all_to_all | solution.py:17
  199.5 0.6 copy-done.8
  (41 shorter events, 1.2 us)
Async XLA Ops:
  0.0 0.8 copy-start.2
  1.5 19.8 %all-to-all-start = ((bf16[16,4,896]{2,1,0:T(4,128)(2,1)}), bf16[16,4,896]{2,1,0:T(4,128)(2,1)S(1)}, u32[]{:S(2)}, u32[]{:S(2)}) async-start(bf16[16,4,896]{2,1,0:T(4,128)(2,1)} %in_columns.1), calls=%async_computation | async-start | bytes 229376 | tf_op jit(solution)/shard_map/all_to_all | solution.py:17
  21.3 81.7 %copy-start = (bf16[1,7168,128]{2,1,0:T(8,128)(2,1)S(1)}, bf16[1,7168,128]{2,1,0:T(8,128)(2,1)}, u32[]{:S(2)}) copy-start(bf16[1,7168,128]{2,1,0:T(8,128)(2,1)} %param.9) | copy-start | bytes 5505028
  62.1 9.8 %collective-permute-start = (bf16[128,896]{1,0:T(8,128)(2,1)S(1)}, bf16[128,896]{1,0:T(8,128)(2,1)S(1)}, u32[]{:S(2)}, u32[]{:S(2)}) collective-permute-start(bf16[128,896]{1,0:T(8,128)(2,1)S(1)} %reshape.46.refs_0_), channel_id=1, source_target_pairs={{0,128},{128,256},{256,384},{384,512},{512,640},{640,768},{768,896... | collective-permute-start | bytes 688136 | tf_op jit(solution)/shard_map/ppermute | solution.py:156
  64.5 9.4 %collective-permute-start.4 = (bf16[128,896]{1,0:T(8,128)(2,1)S(1)}, bf16[128,896]{1,0:T(8,128)(2,1)S(1)}, u32[]{:S(2)}, u32[]{:S(2)}) collective-permute-start(bf16[128,896]{1,0:T(8,128)(2,1)S(1)} %reshape.46.refs_0_), channel_id=1, source_target_pairs={{0,896},{128,0},{256,128},{384,256},{512,384},{640,512},{768,640},... | collective-permute-start | bytes 688136 | tf_op jit(solution)/shard_map/ppermute | solution.py:159
  71.9 9.1 %collective-permute-start.1 = (bf16[128,896]{1,0:T(8,128)(2,1)S(1)}, bf16[128,896]{1,0:T(8,128)(2,1)S(1)}, u32[]{:S(2)}, u32[]{:S(2)}) collective-permute-start(bf16[128,896]{1,0:T(8,128)(2,1)S(1)} %collective-permute-done.refs_0_), channel_id=1, source_target_pairs={{0,128},{128,256},{256,384},{384,512},{512,640},{640,768},{768,896... | collective-permute-start | bytes 688136 | tf_op jit(solution)/shard_map/ppermute | solution.py:156
  73.9 9.1 %collective-permute-start.5 = (bf16[128,896]{1,0:T(8,128)(2,1)S(1)}, bf16[128,896]{1,0:T(8,128)(2,1)S(1)}, u32[]{:S(2)}, u32[]{:S(2)}) collective-permute-start(bf16[128,896]{1,0:T(8,128)(2,1)S(1)} %collective-permute-done.4.refs_0_), channel_id=1, source_target_pairs={{0,896},{128,0},{256,128},{384,256},{512,384},{640,512},{768,640},... | collective-permute-start | bytes 688136 | tf_op jit(solution)/shard_map/ppermute | solution.py:159
  81.0 9.1 %collective-permute-start.2 = (bf16[128,896]{1,0:T(8,128)(2,1)S(1)}, bf16[128,896]{1,0:T(8,128)(2,1)S(1)}, u32[]{:S(2)}, u32[]{:S(2)}) collective-permute-start(bf16[128,896]{1,0:T(8,128)(2,1)S(1)} %collective-permute-done.1.refs_0_), channel_id=1, source_target_pairs={{0,128},{128,256},{256,384},{384,512},{512,640},{640,768},{768,896... | collective-permute-start | bytes 688136 | tf_op jit(solution)/shard_map/ppermute | solution.py:156
  83.0 23.3 %collective-permute-start.6 = (bf16[128,896]{1,0:T(8,128)(2,1)S(1)}, bf16[128,896]{1,0:T(8,128)(2,1)S(1)}, u32[]{:S(2)}, u32[]{:S(2)}) collective-permute-start(bf16[128,896]{1,0:T(8,128)(2,1)S(1)} %collective-permute-done.5.refs_0_), channel_id=1, source_target_pairs={{0,896},{128,0},{256,128},{384,256},{512,384},{640,512},{768,640},... | collective-permute-start | bytes 688136 | tf_op jit(solution)/shard_map/ppermute | solution.py:159
  90.2 17.2 %collective-permute-start.3 = (bf16[128,896]{1,0:T(8,128)(2,1)S(1)}, bf16[128,896]{1,0:T(8,128)(2,1)S(1)}, u32[]{:S(2)}, u32[]{:S(2)}) collective-permute-start(bf16[128,896]{1,0:T(8,128)(2,1)S(1)} %collective-permute-done.2.refs_0_), channel_id=1, source_target_pairs={{0,128},{128,256},{256,384},{384,512},{512,640},{640,768},{768,896... | collective-permute-start | bytes 688136 | tf_op jit(solution)/shard_map/ppermute | solution.py:156
  94.5 0.7 copy-start.3
  95.2 0.7 copy-start.5
  95.9 31.0 %collective-permute-start.10 = (bf16[128,896]{1,0:T(8,128)(2,1)}, bf16[128,896]{1,0:T(8,128)(2,1)S(1)}, u32[]{:S(2)}, u32[]{:S(2)}) collective-permute-start(bf16[128,896]{1,0:T(8,128)(2,1)} %get-tuple-element.49), channel_id=1, source_target_pairs={{0,512},{128,640},{256,768},{384,896},{512,0},{640,128},{768,256},... | collective-permute-start | bytes 688136 | tf_op jit(solution)/shard_map/ppermute | solution.py:174
  98.6 30.2 %collective-permute-start.11 = (bf16[128,896]{1,0:T(8,128)(2,1)}, bf16[128,896]{1,0:T(8,128)(2,1)S(1)}, u32[]{:S(2)}, u32[]{:S(2)}) collective-permute-start(bf16[128,896]{1,0:T(8,128)(2,1)} %get-tuple-element.50), channel_id=1, source_target_pairs={{0,640},{128,768},{256,896},{384,0},{512,128},{640,256},{768,384},... | collective-permute-start | bytes 688136 | tf_op jit(solution)/shard_map/ppermute | solution.py:174
  103.0 1.5 copy-start.1
  107.3 13.7 %copy-start.4 = (bf16[128,896]{1,0:T(8,128)(2,1)S(1)}, bf16[128,896]{1,0:T(8,128)(2,1)}, u32[]{:S(2)}) copy-start(bf16[128,896]{1,0:T(8,128)(2,1)} %copy-done.3) | copy-start | bytes 688132
  108.4 54.7 %copy-start.6 = (s32[1,64,8]{1,2,0:T(8,128)S(1)}, s32[1,64,8]{1,2,0:T(8,128)}, u32[]{:S(2)}) copy-start(s32[1,64,8]{1,2,0:T(8,128)} %param.8) | copy-start | bytes 6148
  108.4 54.8 %copy-start.7 = (s32[1,64,8]{1,2,0:T(8,128)S(1)}, s32[1,64,8]{1,2,0:T(8,128)}, u32[]{:S(2)}) copy-start(s32[1,64,8]{1,2,0:T(8,128)} %param.7) | copy-start | bytes 6148
  108.4 45.0 %all-to-all-start.2 = ((bf16[8,128,128]{2,1,0:T(8,128)(2,1)}), bf16[8,128,128]{2,1,0:T(8,128)(2,1)S(1)}, u32[]{:S(2)}, u32[]{:S(2)}) async-start(bf16[8,128,128]{2,1,0:T(8,128)(2,1)} %broadcast_in_dim.53), calls=%async_computation.2 | async-start | bytes 524288 | tf_op jit(solution)/shard_map/all_to_all | solution.py:17
  114.9 23.9 %collective-permute-start.12 = (bf16[128,896]{1,0:T(8,128)(2,1)}, bf16[128,896]{1,0:T(8,128)(2,1)S(1)}, u32[]{:S(2)}, u32[]{:S(2)}) collective-permute-start(bf16[128,896]{1,0:T(8,128)(2,1)} %copy-done.5), channel_id=1, source_target_pairs={{0,768},{128,896},{256,0},{384,128},{512,256},{640,384},{768,512},... | collective-permute-start | bytes 688136 | tf_op jit(solution)/shard_map/ppermute | solution.py:174
  121.0 21.0 %collective-permute-start.13 = (bf16[128,896]{1,0:T(8,128)(2,1)S(1)}, bf16[128,896]{1,0:T(8,128)(2,1)S(1)}, u32[]{:S(2)}, u32[]{:S(2)}) collective-permute-start(bf16[128,896]{1,0:T(8,128)(2,1)S(1)} %copy-done.4), channel_id=1, source_target_pairs={{0,896},{128,0},{256,128},{384,256},{512,384},{640,512},{768,640},... | collective-permute-start | bytes 688136 | tf_op jit(solution)/shard_map/ppermute | solution.py:174
  124.4 17.6 %collective-permute-start.7 = (bf16[128,896]{1,0:T(8,128)(2,1)S(1)}, bf16[128,896]{1,0:T(8,128)(2,1)S(1)}, u32[]{:S(2)}, u32[]{:S(2)}) collective-permute-start(bf16[128,896]{1,0:T(8,128)(2,1)S(1)} %get-tuple-element.46), channel_id=1, source_target_pairs={{0,128},{128,256},{256,384},{384,512},{512,640},{640,768},{768,896... | collective-permute-start | bytes 688136 | tf_op jit(solution)/shard_map/ppermute | solution.py:174
  126.9 19.6 %collective-permute-start.8 = (bf16[128,896]{1,0:T(8,128)(2,1)S(1)}, bf16[128,896]{1,0:T(8,128)(2,1)S(1)}, u32[]{:S(2)}, u32[]{:S(2)}) collective-permute-start(bf16[128,896]{1,0:T(8,128)(2,1)S(1)} %get-tuple-element.47), channel_id=1, source_target_pairs={{0,256},{128,384},{256,512},{384,640},{512,768},{640,896},{768,0},... | collective-permute-start | bytes 688136 | tf_op jit(solution)/shard_map/ppermute | solution.py:174
  128.8 24.6 %collective-permute-start.9 = (bf16[128,896]{1,0:T(8,128)(2,1)S(1)}, bf16[128,896]{1,0:T(8,128)(2,1)S(1)}, u32[]{:S(2)}, u32[]{:S(2)}) collective-permute-start(bf16[128,896]{1,0:T(8,128)(2,1)S(1)} %get-tuple-element.48), channel_id=1, source_target_pairs={{0,384},{128,512},{256,640},{384,768},{512,896},{640,0},{768,128},... | collective-permute-start | bytes 688136 | tf_op jit(solution)/shard_map/ppermute | solution.py:174
  154.8 29.7 %all-to-all-start.3 = ((bf16[32,4,896]{2,1,0:T(4,128)(2,1)}), bf16[32,4,896]{2,1,0:T(4,128)(2,1)S(1)}, u32[]{:S(2)}, u32[]{:S(2)}) async-start(bf16[32,4,896]{2,1,0:T(4,128)(2,1)} %reshape.47), calls=%async_computation.3 | async-start | bytes 458752 | tf_op jit(solution)/shard_map/all_to_all | solution.py:17
  199.5 0.6 copy-start.8
